TPU v7x, 128 devices: a whole 4x4x4 slice. The times are simulated.
128 devices in a mesh: dp: 8 (over y, x_lo), tensor: 16 (over x_hi, z, core).
Axes of the slice: x: 4 (x_hi: 2, x_lo: 2; x = x_hi * 2 + x_lo), y: 4, z: 4, core: 2. Of those that a mesh axis runs over, the one named last changes fastest.
Arguments:
- grad_out: bfloat16 [8192, 8192], P(('dp', 'tensor')), may hold values from -24 to 24
- out_weight: bfloat16 [8192, 8192], P('dp', 'tensor'), may hold values from -0.0625 to 0.0625
- query: bfloat16 [8192, 8192], P('dp', 'tensor'), may hold values from -6 to 6, as said below
- keys: bfloat16 [8192, 512], P('dp'), may hold values from -6 to 6
- values: bfloat16 [8192, 512], P('dp'), may hold values from -6 to 6
- attended: bfloat16 [8192, 8192], P('dp', 'tensor'), may hold values from -6 to 6, as said below
- stats: float32 [64, 8192], P('tensor', 'dp'), as said below
Outputs:
- query_grad: bfloat16 [8192, 8192], P('dp', 'tensor')
- key_grad: bfloat16 [8192, 512], P('dp', 'tensor')
- value_grad: bfloat16 [8192, 512], P('dp', 'tensor')
- weight_grad: bfloat16 [8192, 8192], P('dp', 'tensor')
Inputs may be any that keep to these rules, and one draw needn't show every extreme that they name: query, keys and values are independent draws. attended is the causal attention output of the given query, keys and values within each sequence of 1024 rows: query head h uses key head h // 16, scores scaled by 128 ** -0.5, softmax over keys at or before the query. stats[h, t] is the logarithm of the sum of exp(score) over the keys that row t of head h attends to, for the same scores.
All inputs are finite; a program needn't handle non-finite values.
Results may differ from a plain program's by a relative error of at most 0.013.
Values may be sent and summed in bfloat16 or wider, within the bound.
No kernel may reach another device: no remote copies, remote signals or barrier semaphores. Data moves between devices by JAX's collectives and lax.ppermute only.
A program may use at most 192 MiB of HBM per device.

v0:
```python
import jax
import jax.numpy as jnp
from jax import lax
from jax.sharding import Mesh
from jax.sharding import PartitionSpec as P

HD = 128
HEAD_DEV = 4
GROUP = 16
DP = ("dp_0", "dp_1")
DP_TENSOR = ("dp_0", "dp_1", "tensor")


def gathered_by_axis(x, axes, dim):
    if not axes:
        return x
    nearer = lax.all_gather(x, axes[-1], axis=dim, tiled=True)
    return gathered_by_axis(nearer, axes[:-1], dim)


def sum_by_axis(terms, axes):
    subtotal = terms.astype(jnp.bfloat16)
    for axis in axes:
        subtotal = lax.psum_scatter(subtotal, axis, scatter_dimension=0, tiled=True)
    return subtotal.astype(jnp.float32)


def partner(value, axis, apart):
    mask = 2**apart
    pairs = [(source, source ^ mask) for source in range(lax.axis_size(axis))]
    return lax.ppermute(value, axis, pairs)


def attention_grads(query, key_one, value_one, attended, grad_att, stats):
    length = query.shape[0]
    score_scale = HD ** (-0.5)
    query_heads = query.reshape(length, HEAD_DEV, HD)
    grad_heads = grad_att.reshape(length, HEAD_DEV, HD)
    attended_heads = attended.reshape(length, HEAD_DEV, HD)
    positions = jnp.arange(length, dtype=jnp.int32)
    causal = positions[:, None] >= positions[None, :]
    scores = (
        jnp.einsum("qgd,kd->gqk", query_heads, key_one, preferred_element_type=jnp.float32)
        * score_scale
    )
    attention = jnp.where(causal[None], jnp.exp(scores - stats[:, :, None]), 0.0)
    attention_low = attention.astype(jnp.bfloat16)
    grad_attention = jnp.einsum(
        "qgd,kd->gqk", grad_heads, value_one, preferred_element_type=jnp.float32
    )
    row_offset = jnp.sum(
        grad_heads.astype(jnp.float32) * attended_heads.astype(jnp.float32), axis=2
    )
    grad_scores = (attention * (grad_attention - row_offset.T[:, :, None])).astype(jnp.bfloat16)
    query_grad = (
        jnp.einsum("gqk,kd->qgd", grad_scores, key_one, preferred_element_type=jnp.float32)
        * score_scale
    )
    query_grad = query_grad.astype(jnp.bfloat16).reshape(length, HEAD_DEV * HD)
    key_part = (
        jnp.einsum("gqk,qgd->kd", grad_scores, query_heads, preferred_element_type=jnp.float32)
        * score_scale
    )
    value_part = jnp.einsum(
        "gqk,qgd->kd", attention_low, grad_heads, preferred_element_type=jnp.float32
    )
    return (query_grad, key_part, value_part)


def per_device(grad_out, out_weight, query, keys, values, attended, stats):
    grad_rows = lax.all_gather(grad_out, "tensor", axis=0, tiled=True)
    grad_block = grad_rows
    grad_att = jnp.dot(
        grad_block, gathered_by_axis(out_weight, DP, 0), preferred_element_type=jnp.float32
    ).astype(jnp.bfloat16)
    grad_block = grad_rows
    weight_grad = sum_by_axis(
        lax.dot_general(
            grad_block, attended, (((0,), (0,)), ((), ())), preferred_element_type=jnp.float32
        ),
        DP,
    ).astype(jnp.bfloat16)
    tensor_index = lax.axis_index("tensor")
    key_head = tensor_index * HEAD_DEV // GROUP
    key_one = lax.dynamic_slice_in_dim(keys, key_head * HD, HD, 1)
    value_one = lax.dynamic_slice_in_dim(values, key_head * HD, HD, 1)
    query_grad, key_part, value_part = attention_grads(
        query, key_one, value_one, attended, grad_att, stats
    )
    group_span = GROUP // HEAD_DEV
    group_place = tensor_index % group_span
    bit_count = group_span.bit_length() - 1
    running_kv = jnp.stack([key_part, value_part])
    for bit_number in reversed(range(bit_count)):
        half_cols = running_kv.shape[2] // 2
        lower_cols = running_kv[:, :, :half_cols]
        upper_cols = running_kv[:, :, half_cols:]
        upper_half = group_place // (1 << bit_number) % 2 == 1
        kept_cols = jnp.where(upper_half, upper_cols, lower_cols)
        sent_cols = jnp.where(upper_half, lower_cols, upper_cols)
        running_kv = kept_cols + partner(
            sent_cols.astype(jnp.bfloat16), "tensor", bit_number
        ).astype(sent_cols.dtype)
    key_grad = running_kv[0].astype(jnp.bfloat16)
    value_grad = running_kv[1].astype(jnp.bfloat16)
    return (query_grad, key_grad, value_grad, weight_grad)


def solution(mesh):
    torus = Mesh(mesh.devices.reshape(4, 2, mesh.shape["tensor"]), ("dp_0", "dp_1", "tensor"))
    in_specs = (
        P(DP_TENSOR, None),
        P(DP, "tensor"),
        P(DP, "tensor"),
        P(DP, None),
        P(DP, None),
        P(DP, "tensor"),
        P("tensor", DP),
    )
    out_specs = (P(DP, "tensor"), P(DP, "tensor"), P(DP, "tensor"), P(DP, "tensor"))
    return jax.shard_map(
        per_device, mesh=torus, in_specs=in_specs, out_specs=out_specs, check_vma=False
    )
```

profile of v0, /device:TPU:1, one launch (start us, length us, event | category | flops | bytes accessed | tf_op | source)
XLA Modules:
  0.0 373.3 jit_solution(7424440204434012823)
XLA Ops:
  7.2 0.0 copy-start
  7.2 0.0 all-gather.6.cloned.1.call-start
  7.2 0.7 all-gather.6.cloned.1.call-update
  7.9 0.0 all-gather.4.cloned.1.call-start
  8.0 0.7 all-gather.4.cloned.1.call-update
  8.7 0.0 all-gather.8.cloned.1.call-start
  8.7 39.6 %all-gather.6.cloned.1.call-done = bf16[2048,512]{1,0:T(8,128)(2,1)} async-done(((bf16[1024,512]{1,0:T(8,128)(2,1)}), bf16[2048,512]{1,0:T(8,128)(2,1)}) %all-gather.6.cloned.1.call-update) | async-done | bytes 2097168 | tf_op jit(solution)/shard_map/all_gather | solution.py:17
  48.3 0.0 all-gather.8.cloned.1.call-update
  48.3 0.0 copy-start.1
  48.3 0.0 copy-start.2
  48.4 0.0 reduce-scatter.3.cloned.1.call-start
  48.4 112.8 %all-gather.4.cloned.1.call-done = bf16[1024,8192]{1,0:T(8,128)(2,1)} async-done(((bf16[64,8192]{1,0:T(8,128)(2,1)}), bf16[1024,8192]{1,0:T(8,128)(2,1)}) %all-gather.4.cloned.1.call-update) | async-done | bytes 16777232 | tf_op jit(solution)/shard_map/all_gather | solution.py:71
  161.2 14.8 %convolution_convert_fusion = bf16[8192,512]{1,0:T(8,128)(2,1)} fusion(bf16[1024,8192]{1,0:T(8,128)(2,1)} %all-gather.4.cloned.1.call-done, bf16[1024,512]{1,0:T(8,128)(2,1)} %param.12), kind=kOutput, calls=%fused_computation.7 | convolution fusion | flops 8594128896 | bytes 26214400 | tf_op jit(solution)/shard_map/dot_general | solution.py:78
  176.0 0.0 reduce-scatter.3.cloned.1.call-update
  176.0 0.2 reduce-scatter.5.cloned.1.call-start
  176.3 0.0 copy-done.1
  176.3 1.6 copy.26
  177.9 0.0 copy-done.2
  177.9 0.5 copy.27
  178.4 0.3 iota_compare_fusion
  178.7 0.0 copy-start.3
  178.8 0.0 copy-done
  178.8 8.1 %fusion.15 = f32[1024,1024,4]{1,0,2:T(8,128)} fusion(bf16[1024,4,128]{0,2,1:T(8,128)(2,1)S(1)} %bitcast.65, bf16[1024,512]{1,0:T(8,128)(2,1)S(1)} %copy-done, s32[]{:T(128)S(6)} %select_n.56), kind=kOutput, calls=%fused_computation.25 | convolution fusion | flops 1073741824 | bytes 18087940 | tf_op jit(solution)/shard_map/qgd,kd->gqk/dot_general | solution.py:43
  186.9 56.2 %all-gather.8.cloned.1.call-done = bf16[8192,512]{1,0:T(8,128)(2,1)} async-done(((bf16[2048,512]{1,0:T(8,128)(2,1)}), bf16[8192,512]{1,0:T(8,128)(2,1)}) %all-gather.8.cloned.1.call-update) | async-done | bytes 8388624 | tf_op jit(solution)/shard_map/all_gather | solution.py:17
  243.0 15.6 %multiply_reduce_fusion = (f32[1024,4]{0,1:T(4,128)S(1)}, bf16[1024,512]{0,1:T(8,128)(2,1)}) fusion(f32[1024,512]{0,1:T(8,128)} %copy.26, bf16[1024,8192]{1,0:T(8,128)(2,1)} %all-gather.4.cloned.1.call-done, bf16[8192,512]{1,0:T(8,128)(2,1)} %all-gather.8.cloned.1.call-done), kind=kOutput, calls=%fused_computation.12 | convolution fusion | flops 8592027648 | bytes 28327936 | tf_op jit(solution)/shard_map/dot_general | solution.py:73
  258.6 68.3 %reduce-scatter.3.cloned.1.call-done = bf16[2048,512]{1,0:T(8,128)(2,1)} async-done(((bf16[8192,512]{1,0:T(8,128)(2,1)}), bf16[2048,512]{1,0:T(8,128)(2,1)}) %reduce-scatter.3.cloned.1.call-update) | async-done | bytes 2097168 | tf_op jit(solution)/shard_map/reduce_scatter | solution.py:24
  326.9 0.0 reduce-scatter.5.cloned.1.call-update
  327.0 0.0 copy-done.3
  327.0 0.0 copy-done.4
  327.0 0.0 slice-start
  327.0 0.0 slice-start.1
  327.0 0.0 slice-start.2
  327.0 0.0 copy-start.5
  327.0 11.5 %fusion.1 = bf16[4,1024,1024]{1,2,0:T(8,128)(2,1)} fusion(f32[1024,1024,4]{1,0,2:T(8,128)} %fusion.15, bf16[1024,4,128]{0,2,1:T(8,128)(2,1)} %bitcast.67, f32[4,1024]{1,0:T(4,128)S(1)} %bitcast.69, f32[4,1024]{1,0:T(4,128)S(1)} %copy-done.4, pred[1024,1024]{0,1:T(8,128)(4,1)S(1)} %iota_compare_fusion, bf16[1024,512]{1,0:T(8,128)(2,1)} %param.11, ...), kind=kOutput, calls=%fused_computation.2 | convolution fusion | flops 1098907648 | bytes 27557892 | tf_op jit(solution)/shard_map/qgd,kd->gqk/dot_general | solution.py:48
  338.5 7.2 %fusion.9 = f32[1,1024,128]{1,2,0:T(8,128)S(1)} fusion(bf16[4,1024,1024]{1,2,0:T(8,128)(2,1)} %fusion.1, bf16[1024,4,128]{0,2,1:T(8,128)(2,1)S(1)} %bitcast.66), kind=kOutput, calls=%fused_computation.16 | convolution fusion | flops 1073872896 | bytes 9961472 | tf_op jit(solution)/shard_map/gqk,qgd->kd/dot_general | solution.py:61
  345.7 0.0 slice-done
  345.7 0.0 slice-done.1
  345.7 0.0 slice-done.2
  345.7 5.2 %fusion.10 = f32[1,1024,128]{1,2,0:T(8,128)S(1)} fusion(bf16[1024,4,128]{0,2,1:T(8,128)(2,1)S(1)} %bitcast.68, f32[1024,1024,4]{1,0,2:T(8,128)S(1)} %bitcast.63, f32[4,1024]{1,0:T(4,128)S(1)} %copy-done.4, pred[1024,1024]{0,1:T(8,128)(4,1)} %copy-done.3), kind=kOutput, calls=%fused_computation.17 | convolution fusion | flops 1090519040 | bytes 19415040 | tf_op jit(solution)/shard_map/gqk,qgd->kd/dot_general | solution.py:64
  351.0 0.1 select_convert_fusion
  351.0 1.5 collective-permute-start
  352.5 6.0 %collective-permute-done = bf16[2,1024,64]{1,2,0:T(8,128)(2,1)S(1)} collective-permute-done((bf16[2,1024,64]{1,2,0:T(8,128)(2,1)S(1)}, bf16[2,1024,64]{1,2,0:T(8,128)(2,1)S(1)}, u32[]{:S(2)}, u32[]{:S(2)}) %collective-permute-start) | collective-permute-done | bytes 262176 | tf_op jit(solution)/shard_map/ppermute | solution.py:31
  358.4 0.1 convert_add_fusion
  358.6 1.5 collective-permute-start.1
  360.0 4.7 %multiply_convert_fusion = bf16[128,4,1024]{2,0,1:T(8,128)(2,1)S(1)} fusion(bf16[4,1024,1024]{1,2,0:T(8,128)(2,1)} %fusion.1, bf16[1024,512]{1,0:T(8,128)(2,1)S(1)} %copy-done, s32[]{:T(128)S(6)} %select_n.56), kind=kOutput, calls=%fused_computation.11 | convolution fusion | flops 1074790400 | bytes 9699332 | tf_op jit(solution)/shard_map/gqk,kd->qgd/dot_general | solution.py:56
  364.7 1.3 copy.19
  366.1 0.0 collective-permute-done.1
  366.1 0.7 slice_bitcast_fusion
  (8 shorter events, 0.1 us)
Async XLA Ops:
  7.2 171.6 %copy-start = (bf16[1024,512]{1,0:T(8,128)(2,1)S(1)}, bf16[1024,512]{1,0:T(8,128)(2,1)}, u32[]{:S(2)}) copy-start(bf16[1024,512]{1,0:T(8,128)(2,1)} %param.10) | copy-start | bytes 3145732
  7.2 41.1 %all-gather.6.cloned.1.call-start = ((), (), s32[]{:S(2)}) async-start(), calls=%async_computation.3 | async-start | bytes 3145728 | tf_op jit(solution)/shard_map/all_gather | solution.py:17
  7.9 153.3 %all-gather.4.cloned.1.call-start = ((), (), s32[]{:S(2)}) async-start(), calls=%async_computation.2 | async-start | bytes 17825792 | tf_op jit(solution)/shard_map/all_gather | solution.py:71
  8.7 234.3 %all-gather.8.cloned.1.call-start = ((), (), s32[]{:S(2)}) async-start(), calls=%async_computation.4 | async-start | bytes 10485760 | tf_op jit(solution)/shard_map/all_gather | solution.py:17
  48.3 127.9 %copy-start.1 = (bf16[1024,512]{1,0:T(8,128)(2,1)S(1)}, bf16[1024,512]{1,0:T(8,128)(2,1)}, u32[]{:S(2)}) copy-start(bf16[1024,512]{1,0:T(8,128)(2,1)} %param.12) | copy-start | bytes 3145732
  48.3 129.5 %copy-start.2 = (bf16[1024,512]{1,0:T(8,128)(2,1)S(1)}, bf16[1024,512]{1,0:T(8,128)(2,1)}, u32[]{:S(2)}) copy-start(bf16[1024,512]{1,0:T(8,128)(2,1)} %param.9) | copy-start | bytes 3145732
  48.4 278.6 %reduce-scatter.3.cloned.1.call-start = ((), (), s32[]{:S(2)}) async-start(), calls=%async_computation.5 | async-start | bytes 10485760 | tf_op jit(solution)/shard_map/reduce_scatter | solution.py:24
  176.0 190.8 %reduce-scatter.5.cloned.1.call-start = ((), (), s32[]{:S(2)}) async-start(), calls=%async_computation.6 | async-start | bytes 3145728 | tf_op jit(solution)/shard_map/reduce_scatter | solution.py:24
  178.7 148.2 %copy-start.3 = (pred[1024,1024]{0,1:T(8,128)(4,1)}, pred[1024,1024]{0,1:T(8,128)(4,1)S(1)}, u32[]{:S(2)}) copy-start(pred[1024,1024]{0,1:T(8,128)(4,1)S(1)} %iota_compare_fusion) | copy-start | bytes 3145732
  186.9 140.1 %copy-start.4 = (f32[4,1024]{1,0:T(4,128)S(1)}, f32[4,1024]{1,0:T(4,128)}, u32[]{:S(2)}) copy-start(f32[4,1024]{1,0:T(4,128)} %param.13) | copy-start | bytes 49156
  327.0 18.7 %slice-start = ((s8[16777216]{0:T(1024)(128)(4,1)}), s8[4194304]{0:T(1024)(128)(4,1)S(1)}, s32[]{:S(2)}) async-start(s8[16777216]{0:T(1024)(128)(4,1)} %bitcast.62), calls=%async_computation.7 | async-start | bytes 8388608
  327.0 18.7 %slice-start.1 = ((s8[16777216]{0:T(1024)(128)(4,1)}), s8[4194304]{0:T(1024)(128)(4,1)S(1)}, s32[]{:S(2)}) async-start(s8[16777216]{0:T(1024)(128)(4,1)} %bitcast.62), calls=%async_computation.8 | async-start | bytes 8388608
  327.0 18.7 %slice-start.2 = ((s8[16777216]{0:T(1024)(128)(4,1)}), s8[4194304]{0:T(1024)(128)(4,1)S(1)}, s32[]{:S(2)}) async-start(s8[16777216]{0:T(1024)(128)(4,1)} %bitcast.62), calls=%async_computation.9 | async-start | bytes 8388608
  327.0 18.7 %copy-start.5 = (bf16[1024,512]{0,1:T(8,128)(2,1)S(1)}, bf16[1024,512]{0,1:T(8,128)(2,1)}, u32[]{:S(2)}) copy-start(bf16[1024,512]{0,1:T(8,128)(2,1)} %get-tuple-element.11) | copy-start | bytes 3145732
  338.5 7.2 %slice-start.3 = ((s8[16777216]{0:T(1024)(128)(4,1)}), s8[4194304]{0:T(1024)(128)(4,1)S(1)}, s32[]{:S(2)}) async-start(s8[16777216]{0:T(1024)(128)(4,1)} %bitcast.62), calls=%async_computation.10 | async-start | bytes 8388608
  351.0 7.4 %collective-permute-start = (bf16[2,1024,64]{1,2,0:T(8,128)(2,1)S(1)}, bf16[2,1024,64]{1,2,0:T(8,128)(2,1)S(1)}, u32[]{:S(2)}, u32[]{:S(2)}) collective-permute-start(bf16[2,1024,64]{1,2,0:T(8,128)(2,1)S(1)} %select_convert_fusion), channel_id=1, source_target_pairs={{0,2},{1,3},{2,0},{3,1},{4,6},{5,7},{6,4},{7,5},{8,10},{9,11},{10,... | collective-permute-start | bytes 786440 | tf_op jit(solution)/shard_map/ppermute | solution.py:31
  358.6 7.5 %collective-permute-start.1 = (bf16[2,1024,32]{1,2,0:T(8,128)(2,1)S(1)}, bf16[2,1024,32]{1,2,0:T(8,128)(2,1)S(1)}, u32[]{:S(2)}, u32[]{:S(2)}) collective-permute-start(bf16[2,1024,32]{1,2,0:T(8,128)(2,1)S(1)} %select_convert_fusion.1), channel_id=1, source_target_pairs={{0,1},{1,0},{2,3},{3,2},{4,5},{5,4},{6,7},{7,6},{8,9},{9,8},{10,11... | collective-permute-start | bytes 393224 | tf_op jit(solution)/shard_map/ppermute | solution.py:31
Sparse Core Ops, SparseCore 0:
  9.6 38.6 all-gather.5
  50.8 110.3 all-gather.3
  162.9 80.0 all-gather.7
  245.3 81.5 reduce-scatter.2
  329.7 34.0 reduce-scatter.4
where the time goes:
time: 373 us
  waiting for transfers between devices  284 us (76%)
  matrix products  67 us (18%)
  between operations  14 us (4%)
  local copies, waits for them, and re-layouts  4.17 us (1%)
    all_gather x1, waiting for transfers between devices, per_device(): grad_rows = lax.all_gather(grad_out, 'tensor', axis=0, tiled=True)  113 us
    all_gather x2, waiting for transfers between devices, gathered_by_axis(): nearer = lax.all_gather(x, axes[-1], axis=dim, tiled=True)  95.7 us
    reduce_scatter x2, waiting for transfers between devices, sum_by_axis(): subtotal = lax.psum_scatter(subtotal, axis, scatter_dimension=0, tiled=True)  68.3 us
    dot_general x1, matrix products, per_device(): jnp.dot(grad_block, gathered_by_axis(out_weight, DP, 0), preferred_elemen...  15.6 us
    dot_general x1, matrix products, per_device(): lax.dot_general(grad_block, attended, (((0,), (0,)), ((), ())), preferred...  14.8 us
    dot_general x1, matrix products, attention_grads(): jnp.einsum('qgd,kd->gqk', grad_heads, value_one, preferred_element_type=j...  11.5 us
    dot_general x1, matrix products, attention_grads(): jnp.einsum('qgd,kd->gqk', query_heads, key_one, preferred_element_type=jn...  8.09 us
  transfers between devices with their start and end apart: 7, of which 5 were waited for; matrix products, arithmetic and copies ran while one was open for 19% of the time, Pallas kernels for 0%

commit v1 on v0

v1 whole, which is shorter than its diff:
```python
import functools

import jax
import jax.numpy as jnp
import numpy as np
from jax import lax
from jax.experimental import pallas as pl
from jax.experimental.pallas import tpu as pltpu
from jax.sharding import Mesh
from jax.sharding import PartitionSpec as P

HD = 128
HEAD_DEV = 4
GROUP = 16
SCALE = HD ** (-0.5)
DP = ("y", "xl")
TENSOR = ("xh", "z", "c")
PIECE = 64
BLOCK = 1024
TOKENS_SEQ = 1024


def swap(x, axis):
    return lax.ppermute(x, axis, [(0, 1), (1, 0)])


def along(x, axis):
    n = lax.axis_size(axis)
    pairs = []
    for i in range(n):
        pairs.append((2 * i, 2 * ((i + 1) % n)))
        pairs.append((2 * i + 1, 2 * ((i - 1) % n) + 1))
    return lax.ppermute(x, (axis, "c"), pairs)


def gather_weight(own):
    def near_blocks(mine):
        other = swap(mine, "c")
        near = along(mine, "y")
        near_other = along(other, "y")
        return [mine, near, swap(near_other, "c")]

    blocks = near_blocks(own)
    far = along(blocks[1], "y")
    partner = swap(own, "xl")
    far_partner = swap(far, "xl")
    return blocks + [far] + near_blocks(partner) + [far_partner]


def weight_order(y, xl, step):
    moved = np.array([0, -1, 1, 2] * 2, np.int32)
    flipped = np.repeat(np.array([0, 1], np.int32), 4)
    return (y + step * moved + 4) % 4 * 2 + (xl + flipped) % 2


def gather_rows(own):
    def ring(mine):
        other = swap(mine, "c")
        near = along(mine, "z")
        near_other = along(other, "z")
        far = along(near, "z")
        return [
            mine,
            other,
            near,
            near_other,
            swap(near, "c"),
            swap(near_other, "c"),
            far,
            swap(far, "c"),
        ]

    partner = swap(own, "xh")
    return ring(own) + ring(partner)


def row_order(xh, z, c, step):
    moved = np.array([0, 0, -1, -1, 1, 1, 2, 2] * 2, np.int32)
    core = np.array([0, 1, 0, 1, 1, 0, 0, 1] * 2, np.int32)
    flipped = np.repeat(np.array([0, 1], np.int32), 8)
    return (xh + flipped) % 2 * 8 + (z + step * moved + 4) % 4 * 2 + (c + core) % 2


def load_rows(pieces, rows):
    for at, piece in enumerate(pieces):
        rows[at * PIECE : (at + 1) * PIECE, :] = piece[...]


def terms_kernel(order, dest, side, *refs, count):
    pieces = refs[:16]
    attended = refs[16:18]
    outs = refs[18 : 18 + count]
    rows, right = refs[18 + count :]
    step = pl.program_id(0)

    @pl.when(step == 0)
    def _():
        for at in range(16):
            start = pl.multiple_of(order[at] * PIECE, PIECE)
            for which in range(2):
                right[which, at * PIECE : (at + 1) * PIECE, :] = attended[which][
                    pl.ds(start, PIECE), :
                ]

    load_rows(pieces, rows)
    total = lax.dot_general(
        rows[...], right[side[step]], (((0,), (0,)), ((), ())), preferred_element_type=jnp.float32
    ).astype(jnp.bfloat16)
    for at in range(count):

        @pl.when(step == at)
        def _():
            outs[at][...] = total


def terms(order, dest, side, pieces, attended, attended_other):
    count = dest.shape[0]
    cols = attended.shape[1]
    whole = pl.BlockSpec((BLOCK, cols), lambda i, order, dest, side: (0, 0))
    piece = pl.BlockSpec((PIECE, BLOCK), lambda i, order, dest, side: (0, dest[i]))
    return pl.pallas_call(
        functools.partial(terms_kernel, count=count),
        grid_spec=pltpu.PrefetchScalarGridSpec(
            num_scalar_prefetch=3,
            grid=(count,),
            in_specs=[piece] * 16 + [whole] * 2,
            out_specs=[whole] * count,
            scratch_shapes=[
                pltpu.VMEM((TOKENS_SEQ, BLOCK), jnp.bfloat16),
                pltpu.VMEM((2, TOKENS_SEQ, cols), jnp.bfloat16),
            ],
        ),
        out_shape=[jax.ShapeDtypeStruct((BLOCK, cols), jnp.bfloat16)] * count,
        cost_estimate=pl.CostEstimate(
            flops=2 * count * BLOCK * cols * TOKENS_SEQ,
            bytes_accessed=count * 3 * 2**20,
            transcendentals=0,
        ),
    )(order, dest, side, *pieces, attended, attended_other)


def dot_kernel(order, place, *refs):
    pieces = refs[:16]
    weights = refs[16:24]
    out, rows, total = refs[24:]
    at_block = pl.program_id(0)
    load_rows(pieces, rows)

    for at in range(8):

        @pl.when(at_block == at)
        def _():
            product = jnp.dot(rows[...], weights[at][...], preferred_element_type=jnp.float32)
            if at == 0:
                total[...] = product
            else:
                total[...] += product

    @pl.when(at_block == 7)
    def _():
        for at in range(16):
            start = pl.multiple_of(order[at] * PIECE, PIECE)
            out[pl.ds(start, PIECE), :] = total[at * PIECE : (at + 1) * PIECE, :].astype(
                jnp.bfloat16
            )


def grad_attention_rows(order, place, pieces, weights):
    cols = weights[0].shape[1]
    return pl.pallas_call(
        dot_kernel,
        grid_spec=pltpu.PrefetchScalarGridSpec(
            num_scalar_prefetch=2,
            grid=(8,),
            in_specs=[pl.BlockSpec((PIECE, BLOCK), lambda i, order, place: (0, place[i]))] * 16
            + [pl.BlockSpec((BLOCK, cols), lambda i, order, place: (0, 0))] * 8,
            out_specs=pl.BlockSpec((TOKENS_SEQ, cols), lambda i, order, place: (0, 0)),
            scratch_shapes=[
                pltpu.VMEM((TOKENS_SEQ, BLOCK), jnp.bfloat16),
                pltpu.VMEM((TOKENS_SEQ, cols), jnp.float32),
            ],
        ),
        out_shape=jax.ShapeDtypeStruct((TOKENS_SEQ, cols), jnp.bfloat16),
        cost_estimate=pl.CostEstimate(
            flops=2 * TOKENS_SEQ * cols * 8 * BLOCK, bytes_accessed=24 * 2**20, transcendentals=0
        ),
    )(order, place, *pieces, *weights)


QB = 256


def head_kernel(query, key, value, grad, attended, stats, query_grad, key_part, value_part):
    head = pl.program_id(0)

    @pl.when(head == 0)
    def _():
        key_part[...] = jnp.zeros_like(key_part)
        value_part[...] = jnp.zeros_like(value_part)

    for block in range(TOKENS_SEQ // QB):
        at = slice(block * QB, (block + 1) * QB)
        seen = (block + 1) * QB
        q = query[at, :]
        g = grad[at, :]
        k = key[:seen, :]
        v = value[:seen, :]
        contract = (((1,), (1,)), ((), ()))
        scores = lax.dot_general(k, q, contract, preferred_element_type=jnp.float32) * SCALE
        attention = jnp.exp(scores - stats[pl.ds(head, 1), at])
        rows = lax.broadcasted_iota(jnp.int32, (seen, QB), 0)
        cols = lax.broadcasted_iota(jnp.int32, (seen, QB), 1) + block * QB
        attention = jnp.where(rows <= cols, attention, 0.0)
        grad_attention = lax.dot_general(v, g, contract, preferred_element_type=jnp.float32)
        offset = g.astype(jnp.float32) * attended[at, :].astype(jnp.float32)
        offset = jnp.sum(offset.T, axis=0, keepdims=True)
        grad_scores = attention * (grad_attention - offset)
        grad_scores = grad_scores.astype(jnp.bfloat16)
        low = attention.astype(jnp.bfloat16)
        value_part[:seen, :] += jnp.dot(low, g, preferred_element_type=jnp.float32)
        key_part[:seen, :] += SCALE * jnp.dot(grad_scores, q, preferred_element_type=jnp.float32)
        back = lax.dot_general(
            grad_scores, k, (((0,), (0,)), ((), ())), preferred_element_type=jnp.float32
        )
        query_grad[at, :] = (back * SCALE).astype(jnp.bfloat16)


def attention_grads(head_at, query, keys, values, grad_att, attended, stats):
    length = query.shape[0]
    column = pl.BlockSpec((length, HD), lambda h, at: (0, h))
    shared = pl.BlockSpec((length, HD), lambda h, at: (0, at[0]))
    row = pl.BlockSpec((HEAD_DEV, length), lambda h, at: (0, 0))
    total = pl.BlockSpec((length, HD), lambda h, at: (0, 0))

    def kernel(at, *refs):
        head_kernel(*refs)

    return pl.pallas_call(
        kernel,
        grid_spec=pltpu.PrefetchScalarGridSpec(
            num_scalar_prefetch=1,
            grid=(HEAD_DEV,),
            in_specs=[column, shared, shared, column, column, row],
            out_specs=[column, total, total],
        ),
        out_shape=[
            jax.ShapeDtypeStruct(query.shape, jnp.bfloat16),
            jax.ShapeDtypeStruct((length, HD), jnp.float32),
            jax.ShapeDtypeStruct((length, HD), jnp.float32),
        ],
        cost_estimate=pl.CostEstimate(
            flops=10 * HEAD_DEV * length * length * HD,
            bytes_accessed=6 * 2**20,
            transcendentals=HEAD_DEV * length * length,
        ),
    )(head_at, query, keys, values, grad_att, attended, stats)


def halved(parts, axis, pairs, upper):
    half = parts.shape[2] // 2
    lower_cols = parts[:, :, :half]
    upper_cols = parts[:, :, half:]
    kept = jnp.where(upper, upper_cols, lower_cols)
    sent = jnp.where(upper, lower_cols, upper_cols)
    got = lax.ppermute(sent.astype(jnp.bfloat16), axis, pairs)
    return kept + got.astype(jnp.float32)


def added(*parts):
    total = parts[0].astype(jnp.float32)
    for part in parts[1:]:
        total = total + part.astype(jnp.float32)
    return total.astype(jnp.bfloat16)


def weight_sums(order, pieces, attended, y, xl, step):
    attended_other = swap(attended, "c")

    def dests(moved, core, flipped):
        moved = np.array(moved, np.int32) + step * np.array(core, np.int32) + 4
        return (y + moved) % 4 * 2 + (xl + np.array(flipped, np.int32)) % 2

    def call(dest, side):
        side = jnp.array(side, jnp.int32)
        return terms(order, dest, side, pieces, attended, attended_other)

    far_p, other_p, near_p, other_o = call(
        dests([2, 0, 0, 0], [0, 1, 1, 1], [1, 1, 1, 0]), [0, 1, 0, 1]
    )
    far_o, near_o, own_p, own_o = call(
        dests([2, 0, 0, 0], [0, 1, 0, 0], [0, 0, 1, 0]), [0, 0, 0, 0]
    )
    far = added(far_o, swap(far_p, "xl"))
    far = along(far, "y")
    near_p = along(near_p, "y")
    near_o = along(added(near_o, far), "y")
    other_p = swap(along(other_p, "y"), "c")
    other_o = swap(along(other_o, "y"), "c")
    partner = swap(added(own_p, near_p, other_p), "xl")
    return added(own_o, other_o, partner, near_o)


def per_device(grad_out, out_weight, query, keys, values, attended, stats):
    y, xl, xh, z, c = (lax.axis_index(name) for name in ("y", "xl", "xh", "z", "c"))
    step = 1 - 2 * c
    pieces = gather_rows(grad_out)
    weights = gather_weight(out_weight)
    order = row_order(xh, z, c, step)
    weight_grad = weight_sums(order, pieces, attended, y, xl, step)
    grad_att = grad_attention_rows(order, weight_order(y, xl, step), pieces, weights)
    key_head = (xh * 8 + z * 2 + c) * HEAD_DEV // GROUP
    query_grad, key_part, value_part = attention_grads(
        key_head.reshape(1), query, keys, values, grad_att, attended, stats
    )
    parts = jnp.stack([key_part, value_part])
    parts = halved(parts, "z", [(0, 1), (1, 0), (2, 3), (3, 2)], z % 2 == 1)
    parts = halved(parts, "c", [(0, 1), (1, 0)], c == 1)
    key_grad = parts[0].astype(jnp.bfloat16)
    value_grad = parts[1].astype(jnp.bfloat16)
    return (query_grad, key_grad, value_grad, weight_grad)


def solution(mesh):
    torus = Mesh(mesh.devices.reshape(4, 2, 2, 4, 2), DP + TENSOR)
    in_specs = (
        P(DP + TENSOR, None),
        P(DP, TENSOR),
        P(DP, TENSOR),
        P(DP, None),
        P(DP, None),
        P(DP, TENSOR),
        P(TENSOR, DP),
    )
    out_specs = (P(DP, TENSOR), P(DP, TENSOR), P(DP, TENSOR), P(DP, TENSOR))
    return jax.shard_map(
        per_device, mesh=torus, in_specs=in_specs, out_specs=out_specs, check_vma=False
    )
```

time: 373 us -> 234 us (0.63)
  waiting for transfers between devices: 284 us -> 103 us
  matrix products: 67 us -> 0 us
  starting transfers between devices: 3.3 us -> 57.4 us
  Pallas kernels: 0 us -> 53.6 us
  other arithmetic: 0.53 us -> 14.4 us
  between operations: 14 us -> 0.82 us
    all_gather x3 -> x0, waiting for transfers between devices: 209 us -> none  [the longest x1 113 us: per_device(): grad_rows = lax.all_gather(grad_out, 'tensor', axis=0, tiled=True)]
    ppermute x2 -> x38, waiting for transfers between devices: 5.96 us -> 103 us  [the longest x16 51.8 us: along(): return lax.ppermute(x, (axis, 'c'), pairs)]
    reduce_scatter x2 -> x0, waiting for transfers between devices: 68.3 us -> none  [sum_by_axis(): subtotal = lax.psum_scatter(subtotal, axis, scatter_dimension=0, tiled=True)]
    dot_general x7 -> x0, matrix products: 67 us -> none  [the longest x1 15.6 us: per_device(): jnp.dot(grad_block, gathered_by_axis(out_weight, DP, 0), preferred_elemen...]
    ppermute x2 -> x38, starting transfers between devices: 2.92 us -> 57.4 us  [the longest x16 32.8 us: along(): return lax.ppermute(x, (axis, 'c'), pairs)]
    pallas_call x0 -> x4, Pallas kernels: none -> 53.6 us  [the longest x2 23.5 us: terms(): pl.pallas_call(functools.partial(terms_kernel, count=count), grid_spec=pl...]
    convert_element_type x2 -> x6, other arithmetic: 0.09 us -> 10.6 us  [the longest x4 8.55 us: added(): return total.astype(jnp.bfloat16)]
  transfers between devices with their start and end apart: 7 -> 38, of which waited for: 5 -> 12; matrix products, arithmetic and copies ran while one was open for 19% -> 7% of each run, Pallas kernels for 0% -> 23%
where the time goes in v1:
time: 234 us
  waiting for transfers between devices  103 us (44%)
  starting transfers between devices  57.4 us (25%)
  Pallas kernels  53.6 us (23%)
  other arithmetic  14.4 us (6%)
  local copies, waits for them, and re-layouts  4.71 us (2%)
    ppermute x16, waiting for transfers between devices, along(): return lax.ppermute(x, (axis, 'c'), pairs)  51.8 us
    ppermute x20, waiting for transfers between devices, swap(): return lax.ppermute(x, axis, [(0, 1), (1, 0)])  43.3 us
    ppermute x16, starting transfers between devices, along(): return lax.ppermute(x, (axis, 'c'), pairs)  32.8 us
    pallas_call x2, Pallas kernels, terms(): pl.pallas_call(functools.partial(terms_kernel, count=count), grid_spec=pl...  23.5 us
    ppermute x20, starting transfers between devices, swap(): return lax.ppermute(x, axis, [(0, 1), (1, 0)])  23.4 us
    pallas_call x1, Pallas kernels, grad_attention_rows(): pl.pallas_call(dot_kernel, grid_spec=pltpu.PrefetchScalarGridSpec(num_sca...  19.5 us
    pallas_call x1, Pallas kernels, attention_grads(): pl.pallas_call(kernel, grid_spec=pltpu.PrefetchScalarGridSpec(num_scalar_...  10.6 us
    convert_element_type x4, other arithmetic, added(): return total.astype(jnp.bfloat16)  8.55 us
  transfers between devices with their start and end apart: 38, of which 12 were waited for; matrix products, arithmetic and copies ran while one was open for 7% of the time, Pallas kernels for 23%

profile of v1, /device:TPU:1, one launch (start us, length us, event | category | flops | bytes accessed | tf_op | source)
XLA Modules:
  0.0 233.8 jit_solution(5564665114796302675)
XLA Ops:
  0.6 3.6 %collective-permute-start.7 = (bf16[64,8192]{1,0:T(8,128)(2,1)}, bf16[64,8192]{1,0:T(8,128)(2,1)S(1)}, u32[]{:S(2)}, u32[]{:S(2)}) collective-permute-start(bf16[64,8192]{1,0:T(8,128)(2,1)} %refs_0_.7), channel_id=1, source_target_pairs={{0,8},{8,0},{1,9},{9,1},{2,10},{10,2},{3,11},{11,3},{4,12},{12,4},... | collective-permute-start | bytes 3145736 | tf_op jit(solution)/shard_map/ppermute | solution.py:24
  4.3 3.8 %collective-permute-start.1 = (bf16[64,8192]{1,0:T(8,128)(2,1)}, bf16[64,8192]{1,0:T(8,128)(2,1)S(1)}, u32[]{:S(2)}, u32[]{:S(2)}) collective-permute-start(bf16[64,8192]{1,0:T(8,128)(2,1)} %refs_0_.7), channel_id=1, source_target_pairs={{0,2},{1,7},{2,4},{3,1},{4,6},{5,3},{6,0},{7,5},{8,10},{9,15},{10,... | collective-permute-start | bytes 3145736 | tf_op jit(solution)/shard_map/ppermute | solution.py:33
  8.9 18.1 %collective-permute-done.7.refs_8_ = bf16[64,8192]{1,0:T(8,128)(2,1)S(1)} collective-permute-done((bf16[64,8192]{1,0:T(8,128)(2,1)}, bf16[64,8192]{1,0:T(8,128)(2,1)S(1)}, u32[]{:S(2)}, u32[]{:S(2)}) %collective-permute-start.7) | collective-permute-done | bytes 1048608 | tf_op jit(solution)/shard_map/ppermute | solution.py:24
  27.0 3.1 %collective-permute-start.15 = (bf16[1024,512]{1,0:T(8,128)(2,1)}, bf16[1024,512]{1,0:T(8,128)(2,1)S(1)}, u32[]{:S(2)}, u32[]{:S(2)}) collective-permute-start(bf16[1024,512]{1,0:T(8,128)(2,1)} %refs_16_.3), channel_id=1, source_target_pairs={{0,32},{1,97},{32,64},{33,1},{64,96},{65,33},{96,0},{97,65},{2,34}... | collective-permute-start | bytes 3145736 | tf_op jit(solution)/shard_map/ppermute | solution.py:33
  30.0 1.5 collective-permute-start.16
  31.5 3.8 %collective-permute-start.9 = (bf16[64,8192]{1,0:T(8,128)(2,1)S(1)}, bf16[64,8192]{1,0:T(8,128)(2,1)}, u32[]{:S(2)}, u32[]{:S(2)}) collective-permute-start(bf16[64,8192]{1,0:T(8,128)(2,1)S(1)} %collective-permute-done.7.refs_8_), channel_id=1, source_target_pairs={{0,2},{1,7},{2,4},{3,1},{4,6},{5,3},{6,0},{7,5},{8,10},{9,15},{10,... | collective-permute-start | bytes 3145736 | tf_op jit(solution)/shard_map/ppermute | solution.py:33
  35.3 14.5 %collective-permute-done.20.refs_20_ = bf16[1024,512]{1,0:T(8,128)(2,1)S(1)} collective-permute-done((bf16[1024,512]{1,0:T(8,128)(2,1)}, bf16[1024,512]{1,0:T(8,128)(2,1)S(1)}, u32[]{:S(2)}, u32[]{:S(2)}) %collective-permute-start.20) | collective-permute-done | bytes 1048608 | tf_op jit(solution)/shard_map/ppermute | solution.py:24
  49.8 3.8 %collective-permute-start.5 = (bf16[64,8192]{1,0:T(8,128)(2,1)S(1)}, bf16[64,8192]{1,0:T(8,128)(2,1)}, u32[]{:S(2)}, u32[]{:S(2)}) collective-permute-start(bf16[64,8192]{1,0:T(8,128)(2,1)S(1)} %collective-permute-done.1.refs_2_), channel_id=1, source_target_pairs={{0,2},{1,7},{2,4},{3,1},{4,6},{5,3},{6,0},{7,5},{8,10},{9,15},{10,... | collective-permute-start | bytes 3145736 | tf_op jit(solution)/shard_map/ppermute | solution.py:33
  53.7 0.9 copy-done.13
  55.4 1.0 collective-permute-start.13
  56.4 8.9 %collective-permute-done.5.refs_6_ = bf16[64,8192]{1,0:T(8,128)(2,1)} collective-permute-done((bf16[64,8192]{1,0:T(8,128)(2,1)S(1)}, bf16[64,8192]{1,0:T(8,128)(2,1)}, u32[]{:S(2)}, u32[]{:S(2)}) %collective-permute-start.5) | collective-permute-done | bytes 1048608 | tf_op jit(solution)/shard_map/ppermute | solution.py:33
  65.3 3.2 %collective-permute-start.10 = (bf16[64,8192]{1,0:T(8,128)(2,1)S(1)}, bf16[64,8192]{1,0:T(8,128)(2,1)}, u32[]{:S(2)}, u32[]{:S(2)}) collective-permute-start(bf16[64,8192]{1,0:T(8,128)(2,1)S(1)} %collective-permute-done.8.refs_9_), channel_id=1, source_target_pairs={{0,2},{1,7},{2,4},{3,1},{4,6},{5,3},{6,0},{7,5},{8,10},{9,15},{10,... | collective-permute-start | bytes 3145736 | tf_op jit(solution)/shard_map/ppermute | solution.py:33
  68.6 8.0 %collective-permute-done.2.refs_3_ = bf16[64,8192]{1,0:T(8,128)(2,1)} collective-permute-done((bf16[64,8192]{1,0:T(8,128)(2,1)S(1)}, bf16[64,8192]{1,0:T(8,128)(2,1)}, u32[]{:S(2)}, u32[]{:S(2)}) %collective-permute-start.2) | collective-permute-done | bytes 1048608 | tf_op jit(solution)/shard_map/ppermute | solution.py:33
  76.6 2.9 %collective-permute-start.11 = (bf16[64,8192]{1,0:T(8,128)(2,1)}, bf16[64,8192]{1,0:T(8,128)(2,1)}, u32[]{:S(2)}, u32[]{:S(2)}) collective-permute-start(bf16[64,8192]{1,0:T(8,128)(2,1)} %collective-permute-done.9.refs_10_), channel_id=1, source_target_pairs={{0,1},{1,0},{2,3},{3,2},{4,5},{5,4},{6,7},{7,6},{8,9},{9,8},{10,11... | collective-permute-start | bytes 3145736 | tf_op jit(solution)/shard_map/ppermute | solution.py:24
  80.1 7.8 %collective-permute-done.13.refs_14_ = bf16[64,8192]{1,0:T(8,128)(2,1)} collective-permute-done((bf16[64,8192]{1,0:T(8,128)(2,1)}, bf16[64,8192]{1,0:T(8,128)(2,1)}, u32[]{:S(2)}, u32[]{:S(2)}) %collective-permute-start.13) | collective-permute-done | bytes 1048608 | tf_op jit(solution)/shard_map/ppermute | solution.py:33
  87.9 2.8 %collective-permute-start.14 = (bf16[64,8192]{1,0:T(8,128)(2,1)}, bf16[64,8192]{1,0:T(8,128)(2,1)}, u32[]{:S(2)}, u32[]{:S(2)}) collective-permute-start(bf16[64,8192]{1,0:T(8,128)(2,1)} %collective-permute-done.13.refs_14_), channel_id=1, source_target_pairs={{0,1},{1,0},{2,3},{3,2},{4,5},{5,4},{6,7},{7,6},{8,9},{9,8},{10,11... | collective-permute-start | bytes 3145736 | tf_op jit(solution)/shard_map/ppermute | solution.py:24
  90.8 8.3 %collective-permute-done.10.refs_11_ = bf16[64,8192]{1,0:T(8,128)(2,1)} collective-permute-done((bf16[64,8192]{1,0:T(8,128)(2,1)S(1)}, bf16[64,8192]{1,0:T(8,128)(2,1)}, u32[]{:S(2)}, u32[]{:S(2)}) %collective-permute-start.10) | collective-permute-done | bytes 1048608 | tf_op jit(solution)/shard_map/ppermute | solution.py:33
  99.1 2.9 %collective-permute-start.12 = (bf16[64,8192]{1,0:T(8,128)(2,1)}, bf16[64,8192]{1,0:T(8,128)(2,1)}, u32[]{:S(2)}, u32[]{:S(2)}) collective-permute-start(bf16[64,8192]{1,0:T(8,128)(2,1)} %collective-permute-done.10.refs_11_), channel_id=1, source_target_pairs={{0,1},{1,0},{2,3},{3,2},{4,5},{5,4},{6,7},{7,6},{8,9},{9,8},{10,11... | collective-permute-start | bytes 3145736 | tf_op jit(solution)/shard_map/ppermute | solution.py:24
  102.0 1.2 fusion.order
  103.2 1.3 fusion.2
  104.6 2.7 %collective-permute-start.19 = (bf16[1024,512]{1,0:T(8,128)(2,1)}, bf16[1024,512]{1,0:T(8,128)(2,1)}, u32[]{:S(2)}, u32[]{:S(2)}) collective-permute-start(bf16[1024,512]{1,0:T(8,128)(2,1)} %copy-done.13), channel_id=1, source_target_pairs={{0,32},{1,97},{32,64},{33,1},{64,96},{65,33},{96,0},{97,65},{2,34}... | collective-permute-start | bytes 3145736 | tf_op jit(solution)/shard_map/ppermute | solution.py:33
  108.0 11.7 %shard_map.222 = (bf16[1024,512]{1,0:T(8,128)(2,1)}, bf16[1024,512]{1,0:T(8,128)(2,1)}, bf16[1024,512]{1,0:T(8,128)(2,1)}, bf16[1024,512]{1,0:T(8,128)(2,1)}) custom-call(s32[16]{0:T(128)} %fusion.order, s32[4]{0:T(128)} %get-tuple-element.33.dest, s32[4]{0:T(128)} %constant.145.clone.side, bf16[64,8192]{1,0:T(8,128)(2,1)} %refs_0_.7, ...), custom_call_target="tpu_custom_call" | custom-call | flops 4294967296 | bytes 12582912 | tf_op jit(solution)/shard_map/pallas_call | solution.py:121
  119.7 1.2 collective-permute-start.35
  121.4 9.1 %collective-permute-done.17 = bf16[1024,512]{1,0:T(8,128)(2,1)} collective-permute-done((bf16[1024,512]{1,0:T(8,128)(2,1)}, bf16[1024,512]{1,0:T(8,128)(2,1)}, u32[]{:S(2)}, u32[]{:S(2)}) %collective-permute-start.17) | collective-permute-done | bytes 1048608 | tf_op jit(solution)/shard_map/ppermute | solution.py:33
  130.6 1.6 collective-permute-start.18
  132.2 9.7 %collective-permute-done.23 = bf16[1024,512]{1,0:T(8,128)(2,1)} collective-permute-done((bf16[1024,512]{1,0:T(8,128)(2,1)}, bf16[1024,512]{1,0:T(8,128)(2,1)}, u32[]{:S(2)}, u32[]{:S(2)}) %collective-permute-start.23) | collective-permute-done | bytes 1048608 | tf_op jit(solution)/shard_map/ppermute | solution.py:33
  141.8 3.1 %collective-permute-start.32 = (bf16[1024,512]{1,0:T(8,128)(2,1)}, bf16[1024,512]{1,0:T(8,128)(2,1)}, u32[]{:S(2)}, u32[]{:S(2)}) collective-permute-start(bf16[1024,512]{1,0:T(8,128)(2,1)} %get-tuple-element.22), channel_id=1, source_target_pairs={{0,32},{1,97},{32,64},{33,1},{64,96},{65,33},{96,0},{97,65},{2,34}... | collective-permute-start | bytes 3145736 | tf_op jit(solution)/shard_map/ppermute | solution.py:33
  144.9 2.2 collective-permute-start.24
  148.3 11.8 %shard_map.221 = (bf16[1024,512]{1,0:T(8,128)(2,1)}, bf16[1024,512]{1,0:T(8,128)(2,1)}, bf16[1024,512]{1,0:T(8,128)(2,1)}, bf16[1024,512]{1,0:T(8,128)(2,1)}) custom-call(s32[16]{0:T(128)} %fusion.order, s32[4]{0:T(128)} %get-tuple-element.32.dest, s32[4]{0:T(128)} %broadcast.66.side, bf16[64,8192]{1,0:T(8,128)(2,1)} %refs_0_.7, bf16[64,8192]{1,0:T(8,128)(2,1)} %copy-done.2, ...), custom_call_target="tpu_custom_call" | custom-call | flops 4294967296 | bytes 12582912 | tf_op jit(solution)/shard_map/pallas_call | solution.py:121
  160.1 1.5 add_convert_fusion.2
  161.6 1.8 collective-permute-start.31
  163.3 2.9 %collective-permute-done.25.refs_23_ = bf16[1024,512]{1,0:T(8,128)(2,1)} collective-permute-done((bf16[1024,512]{1,0:T(8,128)(2,1)}, bf16[1024,512]{1,0:T(8,128)(2,1)}, u32[]{:S(2)}, u32[]{:S(2)}) %collective-permute-start.25) | collective-permute-done | bytes 1048608 | tf_op jit(solution)/shard_map/ppermute | solution.py:24
  166.2 4.0 %collective-permute-start.36 = (bf16[1024,512]{1,0:T(8,128)(2,1)S(1)}, bf16[1024,512]{1,0:T(8,128)(2,1)S(1)}, u32[]{:S(2)}, u32[]{:S(2)}) collective-permute-start(bf16[1024,512]{1,0:T(8,128)(2,1)S(1)} %add_convert_fusion.2), channel_id=1, source_target_pairs={{0,32},{1,97},{32,64},{33,1},{64,96},{65,33},{96,0},{97,65},{2,34}... | collective-permute-start | bytes 3145736 | tf_op jit(solution)/shard_map/ppermute | solution.py:33
  170.2 0.9 collective-permute-start.33
  171.0 19.5 %shard_map.219.refs_3_ = bf16[1024,512]{1,0:T(8,128)(2,1)} custom-call(s32[16]{0:T(128)} %fusion.order, s32[8]{0:T(128)} %fusion.1.place, bf16[64,8192]{1,0:T(8,128)(2,1)} %refs_0_.7, bf16[64,8192]{1,0:T(8,128)(2,1)} %copy-done.2, bf16[64,8192]{1,0:T(8,128)(2,1)} %copy-done.1, bf16[64,8192]{1,0:T(8,128)(2,1)} %collective-permute-done.2.refs_3_, ...), custom_call_target="tpu_custom_call" | custom-call | flops 8589934592 | bytes 25165824 | tf_op jit(solution)/shard_map/pallas_call | solution.py:170
  190.6 10.6 %shard_map.220 = (bf16[1024,512]{1,0:T(8,128)(2,1)}, f32[1024,128]{1,0:T(8,128)}, f32[1024,128]{1,0:T(8,128)}) custom-call(s32[1]{0:T(128)} %bitcast.at, bf16[1024,512]{1,0:T(8,128)(2,1)} %refs_0_.5, bf16[1024,512]{1,0:T(8,128)(2,1)} %refs_1_.1, bf16[1024,512]{1,0:T(8,128)(2,1)} %refs_2_.1, bf16[1024,512]{1,0:T(8,128)(2,1)} %shard_map.219.refs_3_, ...), custom_call_target="tpu_custom_call" | custom-call | flops 5368709120 | bytes 6291456 | tf_op jit(solution)/shard_map/pallas_call | solution.py:238
  201.2 1.8 select_convert_fusion.1
  203.4 3.0 %add_convert_fusion.3 = bf16[1024,512]{1,0:T(8,128)(2,1)} fusion(bf16[1024,512]{1,0:T(8,128)(2,1)} %collective-permute-done.33, bf16[1024,512]{1,0:T(8,128)(2,1)} %collective-permute-done.31, bf16[1024,512]{1,0:T(8,128)(2,1)S(1)} %copy-done.9), kind=kLoop, calls=%fused_computation.3 | loop fusion | flops 3145728 | bytes 4194304 | tf_op jit(solution)/shard_map/convert_element_type | solution.py:273
  206.5 1.1 collective-permute-start.34
  207.6 1.3 add_convert_fusion.1
  208.9 1.7 collective-permute-start.37
  210.6 6.3 %collective-permute-done.26 = bf16[2,1024,64]{2,1,0:T(8,128)(2,1)S(1)} collective-permute-done((bf16[2,1024,64]{2,1,0:T(8,128)(2,1)S(1)}, bf16[2,1024,64]{2,1,0:T(8,128)(2,1)S(1)}, u32[]{:S(2)}, u32[]{:S(2)}) %collective-permute-start.26) | collective-permute-done | bytes 262176 | tf_op jit(solution)/shard_map/ppermute | solution.py:265
  217.4 0.9 collective-permute-start.27
  218.3 1.5 collective-permute-done.27
  220.1 0.8 slice_bitcast_fusion
  220.9 1.7 copy.24
  223.3 7.7 %collective-permute-done.34 = bf16[1024,512]{1,0:T(8,128)(2,1)} collective-permute-done((bf16[1024,512]{1,0:T(8,128)(2,1)}, bf16[1024,512]{1,0:T(8,128)(2,1)}, u32[]{:S(2)}, u32[]{:S(2)}) %collective-permute-start.34) | collective-permute-done | bytes 1048608 | tf_op jit(solution)/shard_map/ppermute | solution.py:24
  231.0 2.8 %add_convert_fusion = bf16[1024,512]{1,0:T(8,128)(2,1)} fusion(bf16[1024,512]{1,0:T(8,128)(2,1)S(1)} %collective-permute-done.37, bf16[1024,512]{1,0:T(8,128)(2,1)} %collective-permute-done.34, bf16[1024,512]{1,0:T(8,128)(2,1)S(1)} %collective-permute-done.30, bf16[1024,512]{1,0:T(8,128)(2,1)S(1)} %copy-done.7), kind=kLoop, calls=%fused_computation | loop fusion | flops 4194304 | bytes 5242880 | tf_op jit(solution)/shard_map/convert_element_type | solution.py:273
  (81 shorter events, 6.7 us)
Async XLA Ops:
  0.6 26.3 %collective-permute-start.7 = (bf16[64,8192]{1,0:T(8,128)(2,1)}, bf16[64,8192]{1,0:T(8,128)(2,1)S(1)}, u32[]{:S(2)}, u32[]{:S(2)}) collective-permute-start(bf16[64,8192]{1,0:T(8,128)(2,1)} %refs_0_.7), channel_id=1, source_target_pairs={{0,8},{8,0},{1,9},{9,1},{2,10},{10,2},{3,11},{11,3},{4,12},{12,4},... | collective-permute-start | bytes 3145736 | tf_op jit(solution)/shard_map/ppermute | solution.py:24
  4.3 25.8 %collective-permute-start.1 = (bf16[64,8192]{1,0:T(8,128)(2,1)}, bf16[64,8192]{1,0:T(8,128)(2,1)S(1)}, u32[]{:S(2)}, u32[]{:S(2)}) collective-permute-start(bf16[64,8192]{1,0:T(8,128)(2,1)} %refs_0_.7), channel_id=1, source_target_pairs={{0,2},{1,7},{2,4},{3,1},{4,6},{5,3},{6,0},{7,5},{8,10},{9,15},{10,... | collective-permute-start | bytes 3145736 | tf_op jit(solution)/shard_map/ppermute | solution.py:33
  8.0 23.5 %collective-permute-start = (bf16[64,8192]{1,0:T(8,128)(2,1)}, bf16[64,8192]{1,0:T(8,128)(2,1)S(1)}, u32[]{:S(2)}, u32[]{:S(2)}) collective-permute-start(bf16[64,8192]{1,0:T(8,128)(2,1)} %refs_0_.7), channel_id=1, source_target_pairs={{0,1},{1,0},{2,3},{3,2},{4,5},{5,4},{6,7},{7,6},{8,9},{9,8},{10,11... | collective-permute-start | bytes 3145736 | tf_op jit(solution)/shard_map/ppermute | solution.py:24
  8.0 27.3 %collective-permute-start.28 = (bf16[1024,512]{1,0:T(8,128)(2,1)}, bf16[1024,512]{1,0:T(8,128)(2,1)}, u32[]{:S(2)}, u32[]{:S(2)}) collective-permute-start(bf16[1024,512]{1,0:T(8,128)(2,1)} %refs_16_.5), channel_id=1, source_target_pairs={{0,1},{1,0},{2,3},{3,2},{4,5},{5,4},{6,7},{7,6},{8,9},{9,8},{10,11... | collective-permute-start | bytes 3145736 | tf_op jit(solution)/shard_map/ppermute | solution.py:24
  8.5 41.3 %collective-permute-start.20 = (bf16[1024,512]{1,0:T(8,128)(2,1)}, bf16[1024,512]{1,0:T(8,128)(2,1)S(1)}, u32[]{:S(2)}, u32[]{:S(2)}) collective-permute-start(bf16[1024,512]{1,0:T(8,128)(2,1)} %refs_16_.3), channel_id=1, source_target_pairs={{0,16},{16,0},{1,17},{17,1},{2,18},{18,2},{3,19},{19,3},{4,20},{20... | collective-permute-start | bytes 3145736 | tf_op jit(solution)/shard_map/ppermute | solution.py:24
  27.0 81.0 %copy-start = (bf16[64,8192]{1,0:T(8,128)(2,1)}, bf16[64,8192]{1,0:T(8,128)(2,1)S(1)}, u32[]{:S(2)}) copy-start(bf16[64,8192]{1,0:T(8,128)(2,1)S(1)} %collective-permute-done.7.refs_8_) | copy-start | bytes 3145732
  27.0 26.6 %collective-permute-start.15 = (bf16[1024,512]{1,0:T(8,128)(2,1)}, bf16[1024,512]{1,0:T(8,128)(2,1)S(1)}, u32[]{:S(2)}, u32[]{:S(2)}) collective-permute-start(bf16[1024,512]{1,0:T(8,128)(2,1)} %refs_16_.3), channel_id=1, source_target_pairs={{0,32},{1,97},{32,64},{33,1},{64,96},{65,33},{96,0},{97,65},{2,34}... | collective-permute-start | bytes 3145736 | tf_op jit(solution)/shard_map/ppermute | solution.py:33
  30.0 77.9 %copy-start.1 = (bf16[64,8192]{1,0:T(8,128)(2,1)}, bf16[64,8192]{1,0:T(8,128)(2,1)S(1)}, u32[]{:S(2)}) copy-start(bf16[64,8192]{1,0:T(8,128)(2,1)S(1)} %collective-permute-done.1.refs_2_) | copy-start | bytes 3145732
  30.0 24.6 %collective-permute-start.16 = (bf16[1024,512]{1,0:T(8,128)(2,1)}, bf16[1024,512]{1,0:T(8,128)(2,1)S(1)}, u32[]{:S(2)}, u32[]{:S(2)}) collective-permute-start(bf16[1024,512]{1,0:T(8,128)(2,1)} %refs_16_.3), channel_id=1, source_target_pairs={{0,1},{1,0},{2,3},{3,2},{4,5},{5,4},{6,7},{7,6},{8,9},{9,8},{10,11... | collective-permute-start | bytes 3145736 | tf_op jit(solution)/shard_map/ppermute | solution.py:24
  31.5 76.4 %copy-start.2 = (bf16[64,8192]{1,0:T(8,128)(2,1)}, bf16[64,8192]{1,0:T(8,128)(2,1)S(1)}, u32[]{:S(2)}) copy-start(bf16[64,8192]{1,0:T(8,128)(2,1)S(1)} %collective-permute-done.refs_1_) | copy-start | bytes 3145732
  31.5 23.8 %collective-permute-start.9 = (bf16[64,8192]{1,0:T(8,128)(2,1)S(1)}, bf16[64,8192]{1,0:T(8,128)(2,1)}, u32[]{:S(2)}, u32[]{:S(2)}) collective-permute-start(bf16[64,8192]{1,0:T(8,128)(2,1)S(1)} %collective-permute-done.7.refs_8_), channel_id=1, source_target_pairs={{0,2},{1,7},{2,4},{3,1},{4,6},{5,3},{6,0},{7,5},{8,10},{9,15},{10,... | collective-permute-start | bytes 3145736 | tf_op jit(solution)/shard_map/ppermute | solution.py:33
  35.3 20.1 %collective-permute-start.8 = (bf16[64,8192]{1,0:T(8,128)(2,1)S(1)}, bf16[64,8192]{1,0:T(8,128)(2,1)S(1)}, u32[]{:S(2)}, u32[]{:S(2)}) collective-permute-start(bf16[64,8192]{1,0:T(8,128)(2,1)S(1)} %collective-permute-done.7.refs_8_), channel_id=1, source_target_pairs={{0,1},{1,0},{2,3},{3,2},{4,5},{5,4},{6,7},{7,6},{8,9},{9,8},{10,11... | collective-permute-start | bytes 3145736 | tf_op jit(solution)/shard_map/ppermute | solution.py:24
  49.8 52.2 %copy-start.12 = (bf16[1024,512]{1,0:T(8,128)(2,1)}, bf16[1024,512]{1,0:T(8,128)(2,1)S(1)}, u32[]{:S(2)}) copy-start(bf16[1024,512]{1,0:T(8,128)(2,1)S(1)} %collective-permute-done.20.refs_20_) | copy-start | bytes 3145732
  49.8 15.5 %collective-permute-start.5 = (bf16[64,8192]{1,0:T(8,128)(2,1)S(1)}, bf16[64,8192]{1,0:T(8,128)(2,1)}, u32[]{:S(2)}, u32[]{:S(2)}) collective-permute-start(bf16[64,8192]{1,0:T(8,128)(2,1)S(1)} %collective-permute-done.1.refs_2_), channel_id=1, source_target_pairs={{0,2},{1,7},{2,4},{3,1},{4,6},{5,3},{6,0},{7,5},{8,10},{9,15},{10,... | collective-permute-start | bytes 3145736 | tf_op jit(solution)/shard_map/ppermute | solution.py:33
  53.6 23.0 %collective-permute-start.2 = (bf16[64,8192]{1,0:T(8,128)(2,1)S(1)}, bf16[64,8192]{1,0:T(8,128)(2,1)}, u32[]{:S(2)}, u32[]{:S(2)}) collective-permute-start(bf16[64,8192]{1,0:T(8,128)(2,1)S(1)} %collective-permute-done.refs_1_), channel_id=1, source_target_pairs={{0,2},{1,7},{2,4},{3,1},{4,6},{5,3},{6,0},{7,5},{8,10},{9,15},{10,... | collective-permute-start | bytes 3145736 | tf_op jit(solution)/shard_map/ppermute | solution.py:33
  54.7 47.3 %copy-start.14 = (bf16[1024,512]{1,0:T(8,128)(2,1)}, bf16[1024,512]{1,0:T(8,128)(2,1)S(1)}, u32[]{:S(2)}) copy-start(bf16[1024,512]{1,0:T(8,128)(2,1)S(1)} %collective-permute-done.16) | copy-start | bytes 3145732
  54.7 24.9 %collective-permute-start.3 = (bf16[64,8192]{1,0:T(8,128)(2,1)S(1)}, bf16[64,8192]{1,0:T(8,128)(2,1)S(1)}, u32[]{:S(2)}, u32[]{:S(2)}) collective-permute-start(bf16[64,8192]{1,0:T(8,128)(2,1)S(1)} %collective-permute-done.1.refs_2_), channel_id=1, source_target_pairs={{0,1},{1,0},{2,3},{3,2},{4,5},{5,4},{6,7},{7,6},{8,9},{9,8},{10,11... | collective-permute-start | bytes 3145736 | tf_op jit(solution)/shard_map/ppermute | solution.py:24
  55.3 24.3 %collective-permute-start.22 = (bf16[1024,512]{1,0:T(8,128)(2,1)S(1)}, bf16[1024,512]{1,0:T(8,128)(2,1)S(1)}, u32[]{:S(2)}, u32[]{:S(2)}) collective-permute-start(bf16[1024,512]{1,0:T(8,128)(2,1)S(1)} %collective-permute-done.20.refs_20_), channel_id=1, source_target_pairs={{0,1},{1,0},{2,3},{3,2},{4,5},{5,4},{6,7},{7,6},{8,9},{9,8},{10,11... | collective-permute-start | bytes 3145736 | tf_op jit(solution)/shard_map/ppermute | solution.py:24
  55.4 24.1 %copy-start.3 = (bf16[64,8192]{1,0:T(8,128)(2,1)}, bf16[64,8192]{1,0:T(8,128)(2,1)S(1)}, u32[]{:S(2)}) copy-start(bf16[64,8192]{1,0:T(8,128)(2,1)S(1)} %collective-permute-done.8.refs_9_) | copy-start | bytes 3145732
  55.4 32.5 %collective-permute-start.13 = (bf16[64,8192]{1,0:T(8,128)(2,1)}, bf16[64,8192]{1,0:T(8,128)(2,1)}, u32[]{:S(2)}, u32[]{:S(2)}) collective-permute-start(bf16[64,8192]{1,0:T(8,128)(2,1)} %collective-permute-done.9.refs_10_), channel_id=1, source_target_pairs={{0,2},{1,7},{2,4},{3,1},{4,6},{5,3},{6,0},{7,5},{8,10},{9,15},{10,... | collective-permute-start | bytes 3145736 | tf_op jit(solution)/shard_map/ppermute | solution.py:33
  65.3 33.7 %collective-permute-start.10 = (bf16[64,8192]{1,0:T(8,128)(2,1)S(1)}, bf16[64,8192]{1,0:T(8,128)(2,1)}, u32[]{:S(2)}, u32[]{:S(2)}) collective-permute-start(bf16[64,8192]{1,0:T(8,128)(2,1)S(1)} %collective-permute-done.8.refs_9_), channel_id=1, source_target_pairs={{0,2},{1,7},{2,4},{3,1},{4,6},{5,3},{6,0},{7,5},{8,10},{9,15},{10,... | collective-permute-start | bytes 3145736 | tf_op jit(solution)/shard_map/ppermute | solution.py:33
  76.6 28.0 %collective-permute-start.11 = (bf16[64,8192]{1,0:T(8,128)(2,1)}, bf16[64,8192]{1,0:T(8,128)(2,1)}, u32[]{:S(2)}, u32[]{:S(2)}) collective-permute-start(bf16[64,8192]{1,0:T(8,128)(2,1)} %collective-permute-done.9.refs_10_), channel_id=1, source_target_pairs={{0,1},{1,0},{2,3},{3,2},{4,5},{5,4},{6,7},{7,6},{8,9},{9,8},{10,11... | collective-permute-start | bytes 3145736 | tf_op jit(solution)/shard_map/ppermute | solution.py:24
  79.5 19.5 %copy-start.4 = (bf16[64,8192]{1,0:T(8,128)(2,1)}, bf16[64,8192]{1,0:T(8,128)(2,1)S(1)}, u32[]{:S(2)}) copy-start(bf16[64,8192]{1,0:T(8,128)(2,1)S(1)} %collective-permute-done.3.refs_4_) | copy-start | bytes 3145732
  79.5 27.8 %collective-permute-start.6 = (bf16[64,8192]{1,0:T(8,128)(2,1)}, bf16[64,8192]{1,0:T(8,128)(2,1)}, u32[]{:S(2)}, u32[]{:S(2)}) collective-permute-start(bf16[64,8192]{1,0:T(8,128)(2,1)} %collective-permute-done.5.refs_6_), channel_id=1, source_target_pairs={{0,1},{1,0},{2,3},{3,2},{4,5},{5,4},{6,7},{7,6},{8,9},{9,8},{10,11... | collective-permute-start | bytes 3145736 | tf_op jit(solution)/shard_map/ppermute | solution.py:24
  79.6 22.4 %copy-start.16 = (bf16[1024,512]{1,0:T(8,128)(2,1)}, bf16[1024,512]{1,0:T(8,128)(2,1)S(1)}, u32[]{:S(2)}) copy-start(bf16[1024,512]{1,0:T(8,128)(2,1)S(1)} %collective-permute-done.22) | copy-start | bytes 3145732
  79.6 28.1 %collective-permute-start.4 = (bf16[64,8192]{1,0:T(8,128)(2,1)}, bf16[64,8192]{1,0:T(8,128)(2,1)}, u32[]{:S(2)}, u32[]{:S(2)}) collective-permute-start(bf16[64,8192]{1,0:T(8,128)(2,1)} %collective-permute-done.2.refs_3_), channel_id=1, source_target_pairs={{0,1},{1,0},{2,3},{3,2},{4,5},{5,4},{6,7},{7,6},{8,9},{9,8},{10,11... | collective-permute-start | bytes 3145736 | tf_op jit(solution)/shard_map/ppermute | solution.py:24
  87.9 20.0 %collective-permute-start.14 = (bf16[64,8192]{1,0:T(8,128)(2,1)}, bf16[64,8192]{1,0:T(8,128)(2,1)}, u32[]{:S(2)}, u32[]{:S(2)}) collective-permute-start(bf16[64,8192]{1,0:T(8,128)(2,1)} %collective-permute-done.13.refs_14_), channel_id=1, source_target_pairs={{0,1},{1,0},{2,3},{3,2},{4,5},{5,4},{6,7},{7,6},{8,9},{9,8},{10,11... | collective-permute-start | bytes 3145736 | tf_op jit(solution)/shard_map/ppermute | solution.py:24
  99.1 8.9 %collective-permute-start.12 = (bf16[64,8192]{1,0:T(8,128)(2,1)}, bf16[64,8192]{1,0:T(8,128)(2,1)}, u32[]{:S(2)}, u32[]{:S(2)}) collective-permute-start(bf16[64,8192]{1,0:T(8,128)(2,1)} %collective-permute-done.10.refs_11_), channel_id=1, source_target_pairs={{0,1},{1,0},{2,3},{3,2},{4,5},{5,4},{6,7},{7,6},{8,9},{9,8},{10,11... | collective-permute-start | bytes 3145736 | tf_op jit(solution)/shard_map/ppermute | solution.py:24
  104.6 16.6 %collective-permute-start.19 = (bf16[1024,512]{1,0:T(8,128)(2,1)}, bf16[1024,512]{1,0:T(8,128)(2,1)}, u32[]{:S(2)}, u32[]{:S(2)}) collective-permute-start(bf16[1024,512]{1,0:T(8,128)(2,1)} %copy-done.13), channel_id=1, source_target_pairs={{0,32},{1,97},{32,64},{33,1},{64,96},{65,33},{96,0},{97,65},{2,34}... | collective-permute-start | bytes 3145736 | tf_op jit(solution)/shard_map/ppermute | solution.py:33
  107.3 23.3 %collective-permute-start.17 = (bf16[1024,512]{1,0:T(8,128)(2,1)}, bf16[1024,512]{1,0:T(8,128)(2,1)}, u32[]{:S(2)}, u32[]{:S(2)}) collective-permute-start(bf16[1024,512]{1,0:T(8,128)(2,1)} %copy-done.14), channel_id=1, source_target_pairs={{0,32},{1,97},{32,64},{33,1},{64,96},{65,33},{96,0},{97,65},{2,34}... | collective-permute-start | bytes 3145736 | tf_op jit(solution)/shard_map/ppermute | solution.py:33
  107.8 34.1 %collective-permute-start.23 = (bf16[1024,512]{1,0:T(8,128)(2,1)}, bf16[1024,512]{1,0:T(8,128)(2,1)}, u32[]{:S(2)}, u32[]{:S(2)}) collective-permute-start(bf16[1024,512]{1,0:T(8,128)(2,1)} %copy-done.16), channel_id=1, source_target_pairs={{0,32},{1,97},{32,64},{33,1},{64,96},{65,33},{96,0},{97,65},{2,34}... | collective-permute-start | bytes 3145736 | tf_op jit(solution)/shard_map/ppermute | solution.py:33
  108.0 39.2 %copy-start.10 = (s32[8]{0:T(128)S(1)}, s32[8]{0:T(128)}, u32[]{:S(2)}) copy-start(s32[8]{0:T(128)} %constant.149.clone) | copy-start | bytes 100
  108.0 39.2 %copy-start.11 = (s32[8]{0:T(128)S(1)}, s32[8]{0:T(128)}, u32[]{:S(2)}) copy-start(s32[8]{0:T(128)} %constant.150.clone) | copy-start | bytes 100
  119.7 25.2 %collective-permute-start.35 = (bf16[1024,512]{1,0:T(8,128)(2,1)}, bf16[1024,512]{1,0:T(8,128)(2,1)S(1)}, u32[]{:S(2)}, u32[]{:S(2)}) collective-permute-start(bf16[1024,512]{1,0:T(8,128)(2,1)} %get-tuple-element.25), channel_id=1, source_target_pairs={{0,16},{16,0},{1,17},{17,1},{2,18},{18,2},{3,19},{19,3},{4,20},{20... | collective-permute-start | bytes 3145736 | tf_op jit(solution)/shard_map/ppermute | solution.py:24
  121.0 40.6 %collective-permute-start.21 = (bf16[1024,512]{1,0:T(8,128)(2,1)}, bf16[1024,512]{1,0:T(8,128)(2,1)S(1)}, u32[]{:S(2)}, u32[]{:S(2)}) collective-permute-start(bf16[1024,512]{1,0:T(8,128)(2,1)} %copy-done.12), channel_id=1, source_target_pairs={{0,32},{1,97},{32,64},{33,1},{64,96},{65,33},{96,0},{97,65},{2,34}... | collective-permute-start | bytes 3145736 | tf_op jit(solution)/shard_map/ppermute | solution.py:33
  121.1 45.1 %collective-permute-start.25 = (bf16[1024,512]{1,0:T(8,128)(2,1)}, bf16[1024,512]{1,0:T(8,128)(2,1)}, u32[]{:S(2)}, u32[]{:S(2)}) collective-permute-start(bf16[1024,512]{1,0:T(8,128)(2,1)} %collective-permute-done.19.refs_19_), channel_id=1, source_target_pairs={{0,16},{16,0},{1,17},{17,1},{2,18},{18,2},{3,19},{19,3},{4,20},{20... | collective-permute-start | bytes 3145736 | tf_op jit(solution)/shard_map/ppermute | solution.py:24
  130.6 35.6 %collective-permute-start.18 = (bf16[1024,512]{1,0:T(8,128)(2,1)}, bf16[1024,512]{1,0:T(8,128)(2,1)}, u32[]{:S(2)}, u32[]{:S(2)}) collective-permute-start(bf16[1024,512]{1,0:T(8,128)(2,1)} %collective-permute-done.17), channel_id=1, source_target_pairs={{0,1},{1,0},{2,3},{3,2},{4,5},{5,4},{6,7},{7,6},{8,9},{9,8},{10,11... | collective-permute-start | bytes 3145736 | tf_op jit(solution)/shard_map/ppermute | solution.py:24
  141.8 28.4 %collective-permute-start.32 = (bf16[1024,512]{1,0:T(8,128)(2,1)}, bf16[1024,512]{1,0:T(8,128)(2,1)}, u32[]{:S(2)}, u32[]{:S(2)}) collective-permute-start(bf16[1024,512]{1,0:T(8,128)(2,1)} %get-tuple-element.22), channel_id=1, source_target_pairs={{0,32},{1,97},{32,64},{33,1},{64,96},{65,33},{96,0},{97,65},{2,34}... | collective-permute-start | bytes 3145736 | tf_op jit(solution)/shard_map/ppermute | solution.py:33
  144.9 26.1 %collective-permute-start.24 = (bf16[1024,512]{1,0:T(8,128)(2,1)}, bf16[1024,512]{1,0:T(8,128)(2,1)}, u32[]{:S(2)}, u32[]{:S(2)}) collective-permute-start(bf16[1024,512]{1,0:T(8,128)(2,1)} %collective-permute-done.23), channel_id=1, source_target_pairs={{0,1},{1,0},{2,3},{3,2},{4,5},{5,4},{6,7},{7,6},{8,9},{9,8},{10,11... | collective-permute-start | bytes 3145736 | tf_op jit(solution)/shard_map/ppermute | solution.py:24
  161.6 41.8 %collective-permute-start.31 = (bf16[1024,512]{1,0:T(8,128)(2,1)}, bf16[1024,512]{1,0:T(8,128)(2,1)}, u32[]{:S(2)}, u32[]{:S(2)}) collective-permute-start(bf16[1024,512]{1,0:T(8,128)(2,1)} %get-tuple-element.21), channel_id=1, source_target_pairs={{0,32},{1,97},{32,64},{33,1},{64,96},{65,33},{96,0},{97,65},{2,34}... | collective-permute-start | bytes 3145736 | tf_op jit(solution)/shard_map/ppermute | solution.py:33
  166.2 37.1 %collective-permute-start.29 = (bf16[1024,512]{1,0:T(8,128)(2,1)}, bf16[1024,512]{1,0:T(8,128)(2,1)}, u32[]{:S(2)}, u32[]{:S(2)}) collective-permute-start(bf16[1024,512]{1,0:T(8,128)(2,1)} %get-tuple-element.19), channel_id=1, source_target_pairs={{0,32},{1,97},{32,64},{33,1},{64,96},{65,33},{96,0},{97,65},{2,34}... | collective-permute-start | bytes 3145736 | tf_op jit(solution)/shard_map/ppermute | solution.py:33
  166.2 41.4 %collective-permute-start.36 = (bf16[1024,512]{1,0:T(8,128)(2,1)S(1)}, bf16[1024,512]{1,0:T(8,128)(2,1)S(1)}, u32[]{:S(2)}, u32[]{:S(2)}) collective-permute-start(bf16[1024,512]{1,0:T(8,128)(2,1)S(1)} %add_convert_fusion.2), channel_id=1, source_target_pairs={{0,32},{1,97},{32,64},{33,1},{64,96},{65,33},{96,0},{97,65},{2,34}... | collective-permute-start | bytes 3145736 | tf_op jit(solution)/shard_map/ppermute | solution.py:33
  170.2 33.2 %collective-permute-start.33 = (bf16[1024,512]{1,0:T(8,128)(2,1)}, bf16[1024,512]{1,0:T(8,128)(2,1)}, u32[]{:S(2)}, u32[]{:S(2)}) collective-permute-start(bf16[1024,512]{1,0:T(8,128)(2,1)} %collective-permute-done.32), channel_id=1, source_target_pairs={{0,1},{1,0},{2,3},{3,2},{4,5},{5,4},{6,7},{7,6},{8,9},{9,8},{10,11... | collective-permute-start | bytes 3145736 | tf_op jit(solution)/shard_map/ppermute | solution.py:24
  203.0 13.8 %collective-permute-start.26 = (bf16[2,1024,64]{2,1,0:T(8,128)(2,1)S(1)}, bf16[2,1024,64]{2,1,0:T(8,128)(2,1)S(1)}, u32[]{:S(2)}, u32[]{:S(2)}) collective-permute-start(bf16[2,1024,64]{2,1,0:T(8,128)(2,1)S(1)} %select_convert_fusion.1), channel_id=1, source_target_pairs={{0,2},{2,0},{4,6},{6,4},{1,3},{3,1},{5,7},{7,5},{8,10},{10,8},{12,... | collective-permute-start | bytes 786440 | tf_op jit(solution)/shard_map/ppermute | solution.py:265
  203.3 20.0 %collective-permute-start.30 = (bf16[1024,512]{1,0:T(8,128)(2,1)}, bf16[1024,512]{1,0:T(8,128)(2,1)S(1)}, u32[]{:S(2)}, u32[]{:S(2)}) collective-permute-start(bf16[1024,512]{1,0:T(8,128)(2,1)} %collective-permute-done.29), channel_id=1, source_target_pairs={{0,1},{1,0},{2,3},{3,2},{4,5},{5,4},{6,7},{7,6},{8,9},{9,8},{10,11... | collective-permute-start | bytes 3145736 | tf_op jit(solution)/shard_map/ppermute | solution.py:24
  206.5 24.6 %collective-permute-start.34 = (bf16[1024,512]{1,0:T(8,128)(2,1)}, bf16[1024,512]{1,0:T(8,128)(2,1)}, u32[]{:S(2)}, u32[]{:S(2)}) collective-permute-start(bf16[1024,512]{1,0:T(8,128)(2,1)} %add_convert_fusion.3), channel_id=1, source_target_pairs={{0,16},{16,0},{1,17},{17,1},{2,18},{18,2},{3,19},{19,3},{4,20},{20... | collective-permute-start | bytes 3145736 | tf_op jit(solution)/shard_map/ppermute | solution.py:24
  208.9 22.2 %collective-permute-start.37 = (bf16[1024,512]{1,0:T(8,128)(2,1)}, bf16[1024,512]{1,0:T(8,128)(2,1)S(1)}, u32[]{:S(2)}, u32[]{:S(2)}) collective-permute-start(bf16[1024,512]{1,0:T(8,128)(2,1)} %add_convert_fusion.1), channel_id=1, source_target_pairs={{0,32},{1,97},{32,64},{33,1},{64,96},{65,33},{96,0},{97,65},{2,34}... | collective-permute-start | bytes 3145736 | tf_op jit(solution)/shard_map/ppermute | solution.py:33
  217.4 2.4 %collective-permute-start.27 = (bf16[2,1024,32]{2,1,0:T(8,128)(2,1)S(1)}, bf16[2,1024,32]{2,1,0:T(8,128)(2,1)S(1)}, u32[]{:S(2)}, u32[]{:S(2)}) collective-permute-start(bf16[2,1024,32]{2,1,0:T(8,128)(2,1)S(1)} %select_convert_fusion), channel_id=1, source_target_pairs={{0,1},{1,0},{2,3},{3,2},{4,5},{5,4},{6,7},{7,6},{8,9},{9,8},{10,11... | collective-permute-start | bytes 393224 | tf_op jit(solution)/shard_map/ppermute | solution.py:265
  (7 other events, 41.5 us)

commit v2 on v1

v2 whole, which is shorter than its diff:
```python
import functools

import jax
import jax.numpy as jnp
import numpy as np
from jax import lax
from jax.experimental import pallas as pl
from jax.experimental.pallas import tpu as pltpu
from jax.sharding import Mesh
from jax.sharding import PartitionSpec as P

HD = 128
HEAD_DEV = 4
GROUP = 16
SCALE = HD ** (-0.5)
DP = ("y", "xl")
TENSOR = ("xh", "z", "c")
PIECE = 64
BLOCK = 1024
AHEAD = 3
SLOTS = AHEAD + 1
TOKENS_SEQ = 1024


def swap(x, axis):
    return lax.ppermute(x, axis, [(0, 1), (1, 0)])


def along(x, axis):
    n = lax.axis_size(axis)
    pairs = []
    for i in range(n):
        pairs.append((2 * i, 2 * ((i + 1) % n)))
        pairs.append((2 * i + 1, 2 * ((i - 1) % n) + 1))
    return lax.ppermute(x, (axis, "c"), pairs)


def gather_weight(own):
    def near_blocks(mine):
        other = swap(mine, "c")
        near = along(mine, "y")
        near_other = along(other, "y")
        return [mine, near, swap(near_other, "c")]

    blocks = near_blocks(own)
    far = along(blocks[1], "y")
    partner = swap(own, "xl")
    far_partner = swap(far, "xl")
    return blocks + [far] + near_blocks(partner) + [far_partner]


def weight_order(y, xl, step):
    moved = np.array([0, -1, 1, 2] * 2, np.int32)
    flipped = np.repeat(np.array([0, 1], np.int32), 4)
    return (y + step * moved + 4) % 4 * 2 + (xl + flipped) % 2


def gather_rows(own):
    def ring(mine):
        other = swap(mine, "c")
        near = along(mine, "z")
        near_other = along(other, "z")
        far = along(near, "z")
        return [
            mine,
            other,
            near,
            near_other,
            swap(near, "c"),
            swap(near_other, "c"),
            far,
            swap(far, "c"),
        ]

    partner = swap(own, "xh")
    return ring(own) + ring(partner)


def row_order(xh, z, c, step):
    moved = np.array([0, 0, -1, -1, 1, 1, 2, 2] * 2, np.int32)
    core = np.array([0, 1, 0, 1, 1, 0, 0, 1] * 2, np.int32)
    flipped = np.repeat(np.array([0, 1], np.int32), 8)
    return (xh + flipped) % 2 * 8 + (z + step * moved + 4) % 4 * 2 + (c + core) % 2


def wait_whole(ref, sem):
    pltpu.make_async_copy(ref, ref, sem).wait()


def fetch_rows(pieces, block, rows, sem):
    start = pl.multiple_of(block * BLOCK, BLOCK)
    for at, piece in enumerate(pieces):
        pltpu.make_async_copy(
            piece.at[:, pl.ds(start, BLOCK)], rows.at[pl.ds(at * PIECE, PIECE), :], sem
        ).start()


def terms_kernel(order, dest, *refs, side):
    count = len(side)
    pieces = refs[:16]
    attended = refs[16:18]
    outs = refs[18 : 18 + count]
    rows, right, made, right_sem, rows_sem, out_sem = refs[18 + count :]
    for which in sorted(set(side)):
        for at in range(16):
            start = pl.multiple_of(order[at] * PIECE, PIECE)
            pltpu.make_async_copy(
                attended[which].at[pl.ds(start, PIECE), :],
                right.at[which, pl.ds(at * PIECE, PIECE), :],
                right_sem.at[which],
            ).start()

    def fetch(at):
        fetch_rows(pieces, dest[at], rows.at[at % SLOTS], rows_sem.at[at % SLOTS])

    for at in range(min(2, count)):
        fetch(at)
    for which in sorted(set(side)):
        wait_whole(right.at[which], right_sem.at[which])
    for at in range(count):
        wait_whole(rows.at[at % SLOTS], rows_sem.at[at % SLOTS])
        if at + 2 < count:
            fetch(at + 2)
        made[at] = lax.dot_general(
            rows[at % SLOTS],
            right[side[at]],
            (((0,), (0,)), ((), ())),
            preferred_element_type=jnp.float32,
        ).astype(jnp.bfloat16)
        pltpu.make_async_copy(made.at[at], outs[at], out_sem.at[at]).start()
    for at in range(count):
        pltpu.make_async_copy(made.at[at], outs[at], out_sem.at[at]).wait()


def terms(order, dest, side, pieces, attended, attended_other):
    count = len(side)
    cols = attended.shape[1]
    small = pl.BlockSpec(memory_space=pltpu.SMEM)
    large = pl.BlockSpec(memory_space=pl.ANY)
    return pl.pallas_call(
        functools.partial(terms_kernel, side=side),
        in_specs=[small] * 2 + [large] * 18,
        out_specs=[large] * count,
        scratch_shapes=[
            pltpu.VMEM((SLOTS, TOKENS_SEQ, BLOCK), jnp.bfloat16),
            pltpu.VMEM((2, TOKENS_SEQ, cols), jnp.bfloat16),
            pltpu.VMEM((count, BLOCK, cols), jnp.bfloat16),
            pltpu.SemaphoreType.DMA((2,)),
            pltpu.SemaphoreType.DMA((SLOTS,)),
            pltpu.SemaphoreType.DMA((count,)),
        ],
        out_shape=[jax.ShapeDtypeStruct((BLOCK, cols), jnp.bfloat16)] * count,
        cost_estimate=pl.CostEstimate(
            flops=2 * count * BLOCK * cols * TOKENS_SEQ,
            bytes_accessed=count * 3 * 2**20,
            transcendentals=0,
        ),
    )(order, dest, *pieces, attended, attended_other)


def dot_kernel(order, place, *refs, jobs, pieces, weights, carried, final):
    count = len(carried)
    piece_refs = refs[:pieces]
    weight_refs = refs[pieces : pieces + weights]
    carried_refs = refs[pieces + weights : pieces + weights + count]
    out, rows, right, total, made, rows_sem, right_sem, carried_sem, out_sem = refs[
        pieces + weights + count :
    ]

    def rows_of(slot, first):
        return rows.at[slot, pl.ds(first * PIECE, (pieces - first) * PIECE), :]

    def fetch(at):
        slot = at % SLOTS
        block, first = jobs[at]
        fetch_rows(
            piece_refs[first:], place[block], rows_of(slot, first), rows_sem.at[slot]
        )
        pltpu.make_async_copy(weight_refs[block], right.at[slot], right_sem.at[slot]).start()

    for at in range(AHEAD):
        fetch(at)
    known = 0
    copies = []
    for at, length in enumerate(carried):
        copies.append(
            pltpu.make_async_copy(
                carried_refs[at], total.at[pl.ds(known, length), :], carried_sem.at[at]
            )
        )
        copies[-1].start()
        known += length
    if known < pieces * PIECE:
        total[known:, :] = jnp.zeros_like(total[known:, :])
    for copy in copies:
        copy.wait()
    for at, (block, first) in enumerate(jobs):
        slot = at % SLOTS
        wait_whole(rows_of(slot, first), rows_sem.at[slot])
        wait_whole(right.at[slot], right_sem.at[slot])
        if at + AHEAD < len(jobs):
            fetch(at + AHEAD)
        total[first * PIECE :, :] += jnp.dot(
            rows[slot, first * PIECE : pieces * PIECE, :],
            right[slot],
            preferred_element_type=jnp.float32,
        )
    if final:
        made[...] = total[...].astype(jnp.bfloat16)
        for at in range(pieces):
            start = pl.multiple_of(order[at] * PIECE, PIECE)
            pltpu.make_async_copy(
                made.at[pl.ds(at * PIECE, PIECE), :], out.at[pl.ds(start, PIECE), :], out_sem
            ).start()
        wait_whole(made, out_sem)
    else:
        copy = pltpu.make_async_copy(total, out, out_sem)
        copy.start()
        copy.wait()


def partial_dot(order, place, pieces, weights, jobs, carried=(), final=False):
    cols = weights[0].shape[1]
    length = len(pieces) * PIECE
    small = pl.BlockSpec(memory_space=pltpu.SMEM)
    large = pl.BlockSpec(memory_space=pl.ANY)
    kernel = functools.partial(
        dot_kernel,
        jobs=jobs,
        pieces=len(pieces),
        weights=len(weights),
        carried=tuple(x.shape[0] for x in carried),
        final=final,
    )
    flops = sum(2 * (len(pieces) - first) * PIECE * BLOCK * cols for _, first in jobs)
    return pl.pallas_call(
        kernel,
        in_specs=[small] * 2 + [large] * (len(pieces) + len(weights) + len(carried)),
        out_specs=large,
        scratch_shapes=[
            pltpu.VMEM((SLOTS, length, BLOCK), jnp.bfloat16),
            pltpu.VMEM((SLOTS, BLOCK, cols), jnp.bfloat16),
            pltpu.VMEM((length, cols), jnp.float32),
            pltpu.VMEM((length if final else PIECE, cols), jnp.bfloat16),
            pltpu.SemaphoreType.DMA((SLOTS,)),
            pltpu.SemaphoreType.DMA((SLOTS,)),
            pltpu.SemaphoreType.DMA((max(len(carried), 1),)),
            pltpu.SemaphoreType.DMA(()),
        ],
        out_shape=jax.ShapeDtypeStruct((length, cols), jnp.bfloat16 if final else jnp.float32),
        cost_estimate=pl.CostEstimate(
            flops=flops, bytes_accessed=len(jobs) * 3 * 2**20, transcendentals=0
        ),
    )(order, place, *pieces, *weights, *carried)


def grad_attention_rows(order, place, pieces, weights):
    early = tuple((block, 0) for block in range(4))
    first = partial_dot(order, place, pieces[:8], weights[:4], early)
    second = partial_dot(order, place, pieces[8:14], weights[:4], early)
    late = tuple((block, 14) for block in range(4)) + tuple((block, 0) for block in range(4, 8))
    return partial_dot(order, place, pieces, weights, late, (first, second), final=True)


QB = 256
QUARTER = HD // 4


def head_kernel(where, *refs, first, count):
    query, key, value, grad, attended, stats = refs[:6]
    step = pl.program_id(0)
    head = step + first
    if first:
        key_start, value_start, _, query_grad, kept, sent, key_part, value_part, sums = refs[6:]
    else:
        query_grad, key_part, value_part = refs[6:]

    @pl.when(step == 0)
    def _():
        key_part[...] = key_start[...] if first else jnp.zeros_like(key_part)
        value_part[...] = value_start[...] if first else jnp.zeros_like(value_part)

    for block in range(TOKENS_SEQ // QB):
        at = slice(block * QB, (block + 1) * QB)
        seen = (block + 1) * QB
        q = query[at, :]
        g = grad[at, :]
        k = key[:seen, :]
        v = value[:seen, :]
        contract = (((1,), (1,)), ((), ()))
        scores = lax.dot_general(k, q, contract, preferred_element_type=jnp.float32) * SCALE
        attention = jnp.exp(scores - stats[pl.ds(head, 1), at])
        rows = lax.broadcasted_iota(jnp.int32, (QB, QB), 0)
        cols = lax.broadcasted_iota(jnp.int32, (QB, QB), 1)
        last = jnp.where(rows <= cols, attention[seen - QB :], 0.0)
        attention = jnp.concatenate([attention[: seen - QB], last], axis=0) if block else last
        grad_attention = lax.dot_general(v, g, contract, preferred_element_type=jnp.float32)
        offset = g.astype(jnp.float32) * attended[at, :].astype(jnp.float32)
        offset = jnp.sum(offset.T, axis=0, keepdims=True)
        grad_scores = attention * (grad_attention - offset)
        grad_scores = grad_scores.astype(jnp.bfloat16)
        low = attention.astype(jnp.bfloat16)
        value_part[:seen, :] += jnp.dot(low, g, preferred_element_type=jnp.float32)
        key_part[:seen, :] += SCALE * jnp.dot(grad_scores, q, preferred_element_type=jnp.float32)
        back = lax.dot_general(
            grad_scores, k, (((0,), (0,)), ((), ())), preferred_element_type=jnp.float32
        )
        query_grad[at, :] = (back * SCALE).astype(jnp.bfloat16)

    if first:

        @pl.when(step == count - 1)
        def _():
            sums[:HD, :] = key_part[...].T
            sums[HD:, :] = value_part[...].T
            for at in range(2 * HD // (2 * QUARTER)):
                rows = slice(at * QUARTER, (at + 1) * QUARTER)
                mine = pl.multiple_of((2 * at + where[1]) * QUARTER, QUARTER)
                other = pl.multiple_of((2 * at + 1 - where[1]) * QUARTER, QUARTER)
                kept[rows, :] = sums[pl.ds(mine, QUARTER), :]
                sent[rows, :] = sums[pl.ds(other, QUARTER), :].astype(jnp.bfloat16)


def attention_grads(head_at, query, keys, values, grad_att, attended, stats):
    length = query.shape[0]
    count = HEAD_DEV // 2
    part = jax.ShapeDtypeStruct((length, HD), jnp.float32)
    scratch = [pltpu.VMEM((length, HD), jnp.float32)] * 2
    scratch += [pltpu.VMEM((2 * HD, length), jnp.float32)]
    whole = pl.BlockSpec((length, HD), lambda h, at: (0, 0))

    def call(first, more):
        column = pl.BlockSpec((length, HD), lambda h, at: (0, h + first))
        shared = pl.BlockSpec((length, HD), lambda h, at: (0, at[0]))
        row = pl.BlockSpec((HEAD_DEV, length), lambda h, at: (0, 0))
        made = [jax.ShapeDtypeStruct(query.shape, jnp.bfloat16)]
        if first:
            made_specs = [column] + [pl.BlockSpec((HD, length), lambda h, at: (0, 0))] * 2
            made += [jax.ShapeDtypeStruct((HD, length), jnp.float32)]
            made += [jax.ShapeDtypeStruct((HD, length), jnp.bfloat16)]
        else:
            made_specs = [column, whole, whole]
            made += [part, part]
        return pl.pallas_call(
            functools.partial(head_kernel, first=first, count=count),
            grid_spec=pltpu.PrefetchScalarGridSpec(
                num_scalar_prefetch=1,
                grid=(count,),
                in_specs=[column, shared, shared, column, column, row]
                + ([whole, whole, pl.BlockSpec(memory_space=pl.ANY)] if first else []),
                out_specs=made_specs,
                scratch_shapes=scratch if first else [],
            ),
            out_shape=made,
            input_output_aliases={9: 0} if first else {},
            cost_estimate=pl.CostEstimate(
                flops=10 * count * length * length * HD,
                bytes_accessed=4 * 2**20,
                transcendentals=count * length * length,
            ),
        )(head_at, query, keys, values, grad_att, attended, stats, *more)

    query_grad, key_part, value_part = call(0, ())
    return call(count, (key_part, value_part, query_grad))


def added(*parts):
    total = parts[0].astype(jnp.float32)
    for part in parts[1:]:
        total = total + part.astype(jnp.float32)
    return total.astype(jnp.bfloat16)


def weight_sums(order, pieces, attended, y, xl, step):
    attended_other = swap(attended, "c")

    def dests(moved, core, flipped):
        moved = np.array(moved, np.int32) + step * np.array(core, np.int32) + 4
        return (y + moved) % 4 * 2 + (xl + np.array(flipped, np.int32)) % 2

    def call(dest, side):
        return terms(order, dest, side, pieces, attended, attended_other)

    other_p, far_p = call(dests([0, 2], [1, 0], [1, 1]), [1, 0])
    near_p, other_o = call(dests([0, 0], [1, 1], [1, 0]), [0, 1])
    far_o, near_o, own_p, own_o = call(
        dests([2, 0, 0, 0], [0, 1, 0, 0], [0, 0, 1, 0]), [0, 0, 0, 0]
    )
    far = added(far_o, swap(far_p, "xl"))
    far = along(far, "y")
    near_p = along(near_p, "y")
    near_o = along(added(near_o, far), "y")
    other_p = swap(along(other_p, "y"), "c")
    other_o = swap(along(other_o, "y"), "c")
    partner = swap(added(own_p, near_p, other_p), "xl")
    known = own_o.astype(jnp.float32) + other_o.astype(jnp.float32)
    known = known + partner.astype(jnp.float32)
    known = lax.optimization_barrier(known)
    return added(known, near_o)


def per_device(grad_out, out_weight, query, keys, values, attended, stats):
    y, xl, xh, z, c = (lax.axis_index(name) for name in ("y", "xl", "xh", "z", "c"))
    step = 1 - 2 * c
    pieces = gather_rows(grad_out)
    weights = gather_weight(out_weight)
    order = row_order(xh, z, c, step)
    weight_grad = weight_sums(order, pieces, attended, y, xl, step)
    grad_att = grad_attention_rows(order, weight_order(y, xl, step), pieces, weights)
    key_head = (xh * 8 + z * 2 + c) * HEAD_DEV // GROUP
    query_grad, kept, sent = attention_grads(
        jnp.stack([key_head, c]), query, keys, values, grad_att, attended, stats
    )
    got = swap(sent, "c")
    parts = (kept + got.astype(jnp.float32)).reshape(2, 2, QUARTER, query.shape[0])
    mine = lax.dynamic_index_in_dim(parts, z % 2, 1, keepdims=False)
    sent = lax.dynamic_index_in_dim(parts, 1 - z % 2, 1, keepdims=False)
    pairs = [(0, 1), (1, 0), (2, 3), (3, 2)]
    got = lax.ppermute(sent.astype(jnp.bfloat16), "z", pairs)
    parts = mine + got.astype(jnp.float32)
    key_grad = parts[0].T.astype(jnp.bfloat16)
    value_grad = parts[1].T.astype(jnp.bfloat16)
    return (query_grad, key_grad, value_grad, weight_grad)


def solution(mesh):
    torus = Mesh(mesh.devices.reshape(4, 2, 2, 4, 2), DP + TENSOR)
    in_specs = (
        P(DP + TENSOR, None),
        P(DP, TENSOR),
        P(DP, TENSOR),
        P(DP, None),
        P(DP, None),
        P(DP, TENSOR),
        P(TENSOR, DP),
    )
    out_specs = (P(DP, TENSOR), P(DP, TENSOR), P(DP, TENSOR), P(DP, TENSOR))
    return jax.shard_map(
        per_device, mesh=torus, in_specs=in_specs, out_specs=out_specs, check_vma=False
    )
```

time: 234 us -> 212 us (0.906)
  waiting for transfers between devices: 103 us -> 86.6 us
  starting transfers between devices: 57.4 us -> 43.6 us
  Pallas kernels: 53.6 us -> 62.2 us
  local copies, waits for them, and re-layouts: 4.71 us -> 0.74 us
  other arithmetic: 14.4 us -> 17.1 us
    ppermute x16, waiting for transfers between devices: 51.8 us -> 33.3 us  [along(): return lax.ppermute(x, (axis, 'c'), pairs)]
    pallas_call x4 -> x8, Pallas kernels: 53.6 us -> 62.2 us  [the longest x3 23.7 us: terms(): pl.pallas_call(functools.partial(terms_kernel, side=side), in_specs=[smal...]
    ppermute x20 -> x21, starting transfers between devices: 23.4 us -> 16.9 us  [swap(): return lax.ppermute(x, axis, [(0, 1), (1, 0)])]
    ppermute x16, starting transfers between devices: 32.8 us -> 26.6 us  [along(): return lax.ppermute(x, (axis, 'c'), pairs)]
    ppermute x20 -> x21, waiting for transfers between devices: 43.3 us -> 48.4 us  [swap(): return lax.ppermute(x, axis, [(0, 1), (1, 0)])]
    unnamed x36, local copies, waits for them, and re-layouts: 3.44 us -> 0.07 us
    ppermute x2 -> x1, waiting for transfers between devices: 7.79 us -> 4.87 us  [per_device(): got = lax.ppermute(sent.astype(jnp.bfloat16), 'z', pairs)]
  transfers between devices with their start and end apart: 38 -> 38, of which waited for: 12 -> 8; matrix products, arithmetic and copies ran while one was open for 7% -> 7% of each run, Pallas kernels for 23% -> 29%
where the time goes in v2:
time: 212 us; the launch traced here: 211 us
  waiting for transfers between devices  86.6 us (41%)
  Pallas kernels  62.2 us (29%)
  starting transfers between devices  43.6 us (21%)
  other arithmetic  17.1 us (8%)
    ppermute x21, waiting for transfers between devices, swap(): return lax.ppermute(x, axis, [(0, 1), (1, 0)])  48.4 us
    ppermute x16, waiting for transfers between devices, along(): return lax.ppermute(x, (axis, 'c'), pairs)  33.3 us
    ppermute x16, starting transfers between devices, along(): return lax.ppermute(x, (axis, 'c'), pairs)  26.6 us
    pallas_call x3, Pallas kernels, terms(): pl.pallas_call(functools.partial(terms_kernel, side=side), in_specs=[smal...  23.7 us
    pallas_call x3, Pallas kernels, partial_dot(): pl.pallas_call(kernel, in_specs=[small] * 2 + [large] * (len(pieces) + le...  23.3 us
    ppermute x21, starting transfers between devices, swap(): return lax.ppermute(x, axis, [(0, 1), (1, 0)])  16.9 us
    pallas_call x2, Pallas kernels, call(): pl.pallas_call(functools.partial(head_kernel, first=first, count=count),...  15.2 us
    convert_element_type x4, other arithmetic, added(): return total.astype(jnp.bfloat16)  9.74 us
  transfers between devices with their start and end apart: 38, of which 8 were waited for; matrix products, arithmetic and copies ran while one was open for 7% of the time, Pallas kernels for 29%

profile of v2, /device:TPU:1, one launch (start us, length us, event | category | flops | bytes accessed | tf_op | source)
XLA Modules:
  0.0 211.2 jit_solution(18060847903293289881)
XLA Ops:
  0.6 1.5 collective-permute-start
  2.1 3.9 %collective-permute-start.1 = (bf16[64,8192]{1,0:T(8,128)(2,1)}, bf16[64,8192]{1,0:T(8,128)(2,1)S(1)}, u32[]{:S(2)}, u32[]{:S(2)}) collective-permute-start(bf16[64,8192]{1,0:T(8,128)(2,1)} %refs_0_.13), channel_id=1, source_target_pairs={{0,2},{1,7},{2,4},{3,1},{4,6},{5,3},{6,0},{7,5},{8,10},{9,15},{10,... | collective-permute-start | bytes 3145736 | tf_op jit(solution)/shard_map/ppermute | solution.py:35
  6.0 2.7 %collective-permute-start.7 = (bf16[64,8192]{1,0:T(8,128)(2,1)}, bf16[64,8192]{1,0:T(8,128)(2,1)S(1)}, u32[]{:S(2)}, u32[]{:S(2)}) collective-permute-start(bf16[64,8192]{1,0:T(8,128)(2,1)} %refs_0_.13), channel_id=1, source_target_pairs={{0,8},{8,0},{1,9},{9,1},{2,10},{10,2},{3,11},{11,3},{4,12},{12,4},... | collective-permute-start | bytes 3145736 | tf_op jit(solution)/shard_map/ppermute | solution.py:26
  8.7 2.7 %collective-permute-start.15 = (bf16[1024,512]{1,0:T(8,128)(2,1)}, bf16[1024,512]{1,0:T(8,128)(2,1)S(1)}, u32[]{:S(2)}, u32[]{:S(2)}) collective-permute-start(bf16[1024,512]{1,0:T(8,128)(2,1)} %refs_16_.4), channel_id=1, source_target_pairs={{0,32},{1,97},{32,64},{33,1},{64,96},{65,33},{96,0},{97,65},{2,34}... | collective-permute-start | bytes 3145736 | tf_op jit(solution)/shard_map/ppermute | solution.py:35
  11.8 6.2 %collective-permute-done.1.refs_2_ = bf16[64,8192]{1,0:T(8,128)(2,1)S(1)} collective-permute-done((bf16[64,8192]{1,0:T(8,128)(2,1)}, bf16[64,8192]{1,0:T(8,128)(2,1)S(1)}, u32[]{:S(2)}, u32[]{:S(2)}) %collective-permute-start.1) | collective-permute-done | bytes 1048608 | tf_op jit(solution)/shard_map/ppermute | solution.py:35
  18.0 1.3 collective-permute-start.28
  19.3 13.2 %collective-permute-done.7.refs_0_.refs_8_ = bf16[64,8192]{1,0:T(8,128)(2,1)S(1)} collective-permute-done((bf16[64,8192]{1,0:T(8,128)(2,1)}, bf16[64,8192]{1,0:T(8,128)(2,1)S(1)}, u32[]{:S(2)}, u32[]{:S(2)}) %collective-permute-start.7) | collective-permute-done | bytes 1048608 | tf_op jit(solution)/shard_map/ppermute | solution.py:26
  32.6 1.3 collective-permute-start.3
  34.0 20.2 %collective-permute-done.20.refs_20_ = bf16[1024,512]{1,0:T(8,128)(2,1)S(1)} collective-permute-done((bf16[1024,512]{1,0:T(8,128)(2,1)}, bf16[1024,512]{1,0:T(8,128)(2,1)S(1)}, u32[]{:S(2)}, u32[]{:S(2)}) %collective-permute-start.20) | collective-permute-done | bytes 1048608 | tf_op jit(solution)/shard_map/ppermute | solution.py:26
  54.2 1.7 collective-permute-start.9
  55.9 2.7 %collective-permute-start.17 = (bf16[1024,512]{1,0:T(8,128)(2,1)S(1)}, bf16[1024,512]{1,0:T(8,128)(2,1)S(1)}, u32[]{:S(2)}, u32[]{:S(2)}) collective-permute-start(bf16[1024,512]{1,0:T(8,128)(2,1)S(1)} %collective-permute-done.16), channel_id=1, source_target_pairs={{0,32},{1,97},{32,64},{33,1},{64,96},{65,33},{96,0},{97,65},{2,34}... | collective-permute-start | bytes 3145736 | tf_op jit(solution)/shard_map/ppermute | solution.py:35
  58.7 0.5 collective-permute-start.19
  59.2 0.6 collective-permute-start.4
  59.7 9.2 %collective-permute-done.9.refs_2_.refs_10_ = bf16[64,8192]{1,0:T(8,128)(2,1)S(1)} collective-permute-done((bf16[64,8192]{1,0:T(8,128)(2,1)S(1)}, bf16[64,8192]{1,0:T(8,128)(2,1)S(1)}, u32[]{:S(2)}, u32[]{:S(2)}) %collective-permute-start.9) | collective-permute-done | bytes 1048608 | tf_op jit(solution)/shard_map/ppermute | solution.py:35
  69.0 2.1 %collective-permute-start.10 = (bf16[64,8192]{1,0:T(8,128)(2,1)S(1)}, bf16[64,8192]{1,0:T(8,128)(2,1)}, u32[]{:S(2)}, u32[]{:S(2)}) collective-permute-start(bf16[64,8192]{1,0:T(8,128)(2,1)S(1)} %collective-permute-done.8.refs_1_.refs_9_), channel_id=1, source_target_pairs={{0,2},{1,7},{2,4},{3,1},{4,6},{5,3},{6,0},{7,5},{8,10},{9,15},{10,... | collective-permute-start | bytes 3145736 | tf_op jit(solution)/shard_map/ppermute | solution.py:35
  71.2 10.5 %collective-permute-done.19.refs_11_.refs_9_.refs_19_ = bf16[1024,512]{1,0:T(8,128)(2,1)S(1)} collective-permute-done((bf16[1024,512]{1,0:T(8,128)(2,1)S(1)}, bf16[1024,512]{1,0:T(8,128)(2,1)S(1)}, u32[]{:S(2)}, u32[]{:S(2)}) %collective-permute-start.19) | collective-permute-done | bytes 1048608 | tf_op jit(solution)/shard_map/ppermute | solution.py:35
  82.2 3.5 %collective-permute-start.23 = (bf16[1024,512]{1,0:T(8,128)(2,1)}, bf16[1024,512]{1,0:T(8,128)(2,1)}, u32[]{:S(2)}, u32[]{:S(2)}) collective-permute-start(bf16[1024,512]{1,0:T(8,128)(2,1)} %collective-permute-done.22), channel_id=1, source_target_pairs={{0,32},{1,97},{32,64},{33,1},{64,96},{65,33},{96,0},{97,65},{2,34}... | collective-permute-start | bytes 3145736 | tf_op jit(solution)/shard_map/ppermute | solution.py:35
  85.7 1.2 collective-permute-start.12
  86.9 7.4 %collective-permute-done.13.refs_14_ = bf16[64,8192]{1,0:T(8,128)(2,1)} collective-permute-done((bf16[64,8192]{1,0:T(8,128)(2,1)S(1)}, bf16[64,8192]{1,0:T(8,128)(2,1)}, u32[]{:S(2)}, u32[]{:S(2)}) %collective-permute-start.13) | collective-permute-done | bytes 1048608 | tf_op jit(solution)/shard_map/ppermute | solution.py:35
  94.3 3.8 %collective-permute-start.14 = (bf16[64,8192]{1,0:T(8,128)(2,1)}, bf16[64,8192]{1,0:T(8,128)(2,1)}, u32[]{:S(2)}, u32[]{:S(2)}) collective-permute-start(bf16[64,8192]{1,0:T(8,128)(2,1)} %collective-permute-done.13.refs_14_), channel_id=1, source_target_pairs={{0,1},{1,0},{2,3},{3,2},{4,5},{5,4},{6,7},{7,6},{8,9},{9,8},{10,11... | collective-permute-start | bytes 3145736 | tf_op jit(solution)/shard_map/ppermute | solution.py:26
  98.3 1.3 fusion.3.place
  99.6 1.2 fusion.2.order
  100.8 1.2 fusion.4.dest
  102.0 2.7 %collective-permute-start.21 = (bf16[1024,512]{1,0:T(8,128)(2,1)}, bf16[1024,512]{1,0:T(8,128)(2,1)}, u32[]{:S(2)}, u32[]{:S(2)}) collective-permute-start(bf16[1024,512]{1,0:T(8,128)(2,1)} %copy-done.11), channel_id=1, source_target_pairs={{0,32},{1,97},{32,64},{33,1},{64,96},{65,33},{96,0},{97,65},{2,34}... | collective-permute-start | bytes 3145736 | tf_op jit(solution)/shard_map/ppermute | solution.py:35
  104.7 1.2 collective-permute-start.25
  105.9 1.3 fusion.12
  107.2 7.2 %shard_map.235 = (bf16[1024,512]{1,0:T(8,128)(2,1)}, bf16[1024,512]{1,0:T(8,128)(2,1)}) custom-call(s32[16]{0:T(128)} %fusion.2.order, s32[2]{0:T(128)} %get-tuple-element.35.dest, bf16[64,8192]{1,0:T(8,128)(2,1)} %refs_0_.13, bf16[64,8192]{1,0:T(8,128)(2,1)} %copy-done.3, bf16[64,8192]{1,0:T(8,128)(2,1)} %copy-done.4, bf16[64,8192]{1,0:T(8,128)(2,1)} %copy-done.5, ...), custom_call_target="tpu_custom_call" | custom-call | flops 2147483648 | bytes 6291456 | tf_op jit(solution)/shard_map/pallas_call | solution.py:140
  114.3 1.2 collective-permute-start.32
  115.6 0.7 pad_add_fusion.where
  116.2 6.5 %shard_map.228.refs_24_ = f32[512,512]{1,0:T(8,128)} custom-call(s32[16]{0:T(128)} %fusion.2.order, s32[8]{0:T(128)} %fusion.3.place, bf16[64,8192]{1,0:T(8,128)(2,1)} %refs_0_.13, bf16[64,8192]{1,0:T(8,128)(2,1)} %copy-done.3, bf16[64,8192]{1,0:T(8,128)(2,1)} %copy-done.4, bf16[64,8192]{1,0:T(8,128)(2,1)} %copy-done.5, bf16[64,8192]{1,0:T(8,128)(2,1)} %copy-done.6, ...), custom_call_target="tpu_custom_call" | custom-call | flops 2147483648 | bytes 12582912 | tf_op jit(solution)/shard_map/pallas_call | solution.py:236
  123.2 5.7 %shard_map.229.refs_25_ = f32[384,512]{1,0:T(8,128)} custom-call(s32[16]{0:T(128)} %fusion.2.order, s32[8]{0:T(128)} %fusion.3.place, bf16[64,8192]{1,0:T(8,128)(2,1)} %copy-done, bf16[64,8192]{1,0:T(8,128)(2,1)} %copy-done.1, bf16[64,8192]{1,0:T(8,128)(2,1)} %copy-done.2, bf16[64,8192]{1,0:T(8,128)(2,1)} %collective-permute-done.10.refs_3_.refs_11_, ...), custom_call_target="tpu_custom_call" | custom-call | flops 1610612736 | bytes 12582912 | tf_op jit(solution)/shard_map/pallas_call | solution.py:236
  128.9 7.1 %shard_map.234 = (bf16[1024,512]{1,0:T(8,128)(2,1)}, bf16[1024,512]{1,0:T(8,128)(2,1)}) custom-call(s32[16]{0:T(128)} %fusion.2.order, s32[2]{0:T(128)} %get-tuple-element.34.dest, bf16[64,8192]{1,0:T(8,128)(2,1)} %refs_0_.13, bf16[64,8192]{1,0:T(8,128)(2,1)} %copy-done.3, bf16[64,8192]{1,0:T(8,128)(2,1)} %copy-done.4, bf16[64,8192]{1,0:T(8,128)(2,1)} %copy-done.5, ...), custom_call_target="tpu_custom_call" | custom-call | flops 2147483648 | bytes 6291456 | tf_op jit(solution)/shard_map/pallas_call | solution.py:140
  136.1 1.6 collective-permute-start.31
  138.1 11.0 %shard_map.230.refs_3_ = bf16[1024,512]{1,0:T(8,128)(2,1)} custom-call(s32[16]{0:T(128)} %fusion.2.order, s32[8]{0:T(128)} %fusion.3.place, bf16[64,8192]{1,0:T(8,128)(2,1)} %refs_0_.13, bf16[64,8192]{1,0:T(8,128)(2,1)} %copy-done.3, bf16[64,8192]{1,0:T(8,128)(2,1)} %copy-done.4, bf16[64,8192]{1,0:T(8,128)(2,1)} %copy-done.5, bf16[64,8192]{1,0:T(8,128)(2,1)} %copy-done.6, ...), custom_call_target="tpu_custom_call" | custom-call | flops 4831838208 | bytes 25165824 | tf_op jit(solution)/shard_map/pallas_call | solution.py:236
  149.5 9.4 %shard_map.233 = (bf16[1024,512]{1,0:T(8,128)(2,1)}, bf16[1024,512]{1,0:T(8,128)(2,1)}, bf16[1024,512]{1,0:T(8,128)(2,1)}, bf16[1024,512]{1,0:T(8,128)(2,1)}) custom-call(s32[16]{0:T(128)} %fusion.2.order, s32[4]{0:T(128)} %fusion.4.dest, bf16[64,8192]{1,0:T(8,128)(2,1)} %refs_0_.13, bf16[64,8192]{1,0:T(8,128)(2,1)} %copy-done.3, ...), custom_call_target="tpu_custom_call" | custom-call | flops 4294967296 | bytes 12582912 | tf_op jit(solution)/shard_map/pallas_call | solution.py:140
  158.9 1.5 add_convert_fusion.2
  160.4 2.8 %collective-permute-start.36 = (bf16[1024,512]{1,0:T(8,128)(2,1)S(1)}, bf16[1024,512]{1,0:T(8,128)(2,1)}, u32[]{:S(2)}, u32[]{:S(2)}) collective-permute-start(bf16[1024,512]{1,0:T(8,128)(2,1)S(1)} %add_convert_fusion.2), channel_id=1, source_target_pairs={{0,32},{1,97},{32,64},{33,1},{64,96},{65,33},{96,0},{97,65},{2,34}... | collective-permute-start | bytes 3145736 | tf_op jit(solution)/shard_map/ppermute | solution.py:35
  163.2 7.1 %shard_map.231 = (bf16[1024,512]{1,0:T(8,128)(2,1)}, f32[1024,128]{1,0:T(8,128)}, f32[1024,128]{1,0:T(8,128)}) custom-call(s32[2]{0:T(128)} %pad_add_fusion.where, bf16[1024,512]{1,0:T(8,128)(2,1)} %refs_0_.10, bf16[1024,512]{1,0:T(8,128)(2,1)} %refs_1_.3, bf16[1024,512]{1,0:T(8,128)(2,1)} %refs_2_.3, bf16[1024,512]{1,0:T(8,128)(2,1)} %shard_map.230.refs_3_, ...), custom_call_target="tpu_custom_call" | custom-call | flops 2684354560 | bytes 4194304 | tf_op jit(solution)/shard_map/pallas_call | solution.py:344
  170.3 8.1 %shard_map.232 = (bf16[1024,512]{1,0:T(8,128)(2,1)}, f32[128,1024]{1,0:T(8,128)}, bf16[128,1024]{1,0:T(8,128)(2,1)}) custom-call(s32[2]{0:T(128)} %pad_add_fusion.where, bf16[1024,512]{1,0:T(8,128)(2,1)} %refs_0_.10, bf16[1024,512]{1,0:T(8,128)(2,1)} %refs_1_.3, bf16[1024,512]{1,0:T(8,128)(2,1)} %refs_2_.3, ...), custom_call_target="tpu_custom_call", output_to_operand_aliasing={{0}: (9, {})} | custom-call | flops 2684354560 | bytes 4194304 | tf_op jit(solution)/shard_map/pallas_call | solution.py:344
  178.5 0.5 collective-permute-start.30
  179.0 3.0 %add_convert_fusion.3 = bf16[1024,512]{1,0:T(8,128)(2,1)} fusion(bf16[1024,512]{1,0:T(8,128)(2,1)} %collective-permute-done.33, bf16[1024,512]{1,0:T(8,128)(2,1)} %collective-permute-done.31, bf16[1024,512]{1,0:T(8,128)(2,1)S(1)} %copy-done.14), kind=kLoop, calls=%fused_computation.4 | loop fusion | flops 3145728 | bytes 4194304 | tf_op jit(solution)/shard_map/convert_element_type | solution.py:371
  182.0 1.2 collective-permute-start.34
  183.3 2.6 %add_convert_fusion.1 = bf16[1024,512]{1,0:T(8,128)(2,1)} fusion(bf16[1024,512]{1,0:T(8,128)(2,1)} %collective-permute-done.36, bf16[1024,512]{1,0:T(8,128)(2,1)S(1)} %copy-done.13), kind=kLoop, calls=%fused_computation.1 | loop fusion | flops 2097152 | bytes 3145728 | tf_op jit(solution)/shard_map/convert_element_type | solution.py:371
  186.5 4.9 %collective-permute-done.27 = bf16[2,32,1024]{2,1,0:T(8,128)(2,1)S(1)} collective-permute-done((bf16[2,32,1024]{2,1,0:T(8,128)(2,1)S(1)}, bf16[2,32,1024]{2,1,0:T(8,128)(2,1)S(1)}, u32[]{:S(2)}, u32[]{:S(2)}) %collective-permute-start.27) | collective-permute-done | bytes 131104 | tf_op jit(solution)/shard_map/ppermute | solution.py:419
  191.4 0.7 slice_bitcast_fusion
  192.1 14.9 %collective-permute-done.34 = bf16[1024,512]{1,0:T(8,128)(2,1)} collective-permute-done((bf16[1024,512]{1,0:T(8,128)(2,1)}, bf16[1024,512]{1,0:T(8,128)(2,1)}, u32[]{:S(2)}, u32[]{:S(2)}) %collective-permute-start.34) | collective-permute-done | bytes 1048608 | tf_op jit(solution)/shard_map/ppermute | solution.py:26
  207.0 1.6 convert_add_fusion
  208.6 2.6 %add_convert_fusion = bf16[1024,512]{1,0:T(8,128)(2,1)} fusion(f32[1024,512]{1,0:T(8,128)S(1)} %convert_add_fusion, bf16[1024,512]{1,0:T(8,128)(2,1)} %collective-permute-done.37), kind=kLoop, calls=%fused_computation | loop fusion | flops 1572864 | bytes 4194304 | tf_op jit(solution)/shard_map/convert_element_type | solution.py:371
  (86 shorter events, 3.2 us)
Async XLA Ops:
  0.6 10.8 %collective-permute-start = (bf16[64,8192]{1,0:T(8,128)(2,1)}, bf16[64,8192]{1,0:T(8,128)(2,1)S(1)}, u32[]{:S(2)}, u32[]{:S(2)}) collective-permute-start(bf16[64,8192]{1,0:T(8,128)(2,1)} %refs_0_.13), channel_id=1, source_target_pairs={{0,1},{1,0},{2,3},{3,2},{4,5},{5,4},{6,7},{7,6},{8,9},{9,8},{10,11... | collective-permute-start | bytes 3145736 | tf_op jit(solution)/shard_map/ppermute | solution.py:26
  2.1 15.9 %collective-permute-start.1 = (bf16[64,8192]{1,0:T(8,128)(2,1)}, bf16[64,8192]{1,0:T(8,128)(2,1)S(1)}, u32[]{:S(2)}, u32[]{:S(2)}) collective-permute-start(bf16[64,8192]{1,0:T(8,128)(2,1)} %refs_0_.13), channel_id=1, source_target_pairs={{0,2},{1,7},{2,4},{3,1},{4,6},{5,3},{6,0},{7,5},{8,10},{9,15},{10,... | collective-permute-start | bytes 3145736 | tf_op jit(solution)/shard_map/ppermute | solution.py:35
  6.0 26.6 %collective-permute-start.7 = (bf16[64,8192]{1,0:T(8,128)(2,1)}, bf16[64,8192]{1,0:T(8,128)(2,1)S(1)}, u32[]{:S(2)}, u32[]{:S(2)}) collective-permute-start(bf16[64,8192]{1,0:T(8,128)(2,1)} %refs_0_.13), channel_id=1, source_target_pairs={{0,8},{8,0},{1,9},{9,1},{2,10},{10,2},{3,11},{11,3},{4,12},{12,4},... | collective-permute-start | bytes 3145736 | tf_op jit(solution)/shard_map/ppermute | solution.py:26
  8.7 23.9 %collective-permute-start.15 = (bf16[1024,512]{1,0:T(8,128)(2,1)}, bf16[1024,512]{1,0:T(8,128)(2,1)S(1)}, u32[]{:S(2)}, u32[]{:S(2)}) collective-permute-start(bf16[1024,512]{1,0:T(8,128)(2,1)} %refs_16_.4), channel_id=1, source_target_pairs={{0,32},{1,97},{32,64},{33,1},{64,96},{65,33},{96,0},{97,65},{2,34}... | collective-permute-start | bytes 3145736 | tf_op jit(solution)/shard_map/ppermute | solution.py:35
  11.4 22.4 %collective-permute-start.16 = (bf16[1024,512]{1,0:T(8,128)(2,1)}, bf16[1024,512]{1,0:T(8,128)(2,1)S(1)}, u32[]{:S(2)}, u32[]{:S(2)}) collective-permute-start(bf16[1024,512]{1,0:T(8,128)(2,1)} %refs_16_.4), channel_id=1, source_target_pairs={{0,1},{1,0},{2,3},{3,2},{4,5},{5,4},{6,7},{7,6},{8,9},{9,8},{10,11... | collective-permute-start | bytes 3145736 | tf_op jit(solution)/shard_map/ppermute | solution.py:26
  11.4 82.8 %copy-start.3 = (bf16[64,8192]{1,0:T(8,128)(2,1)}, bf16[64,8192]{1,0:T(8,128)(2,1)S(1)}, u32[]{:S(2)}) copy-start(bf16[64,8192]{1,0:T(8,128)(2,1)S(1)} %collective-permute-done.refs_1_) | copy-start | bytes 3145732
  11.5 42.8 %collective-permute-start.20 = (bf16[1024,512]{1,0:T(8,128)(2,1)}, bf16[1024,512]{1,0:T(8,128)(2,1)S(1)}, u32[]{:S(2)}, u32[]{:S(2)}) collective-permute-start(bf16[1024,512]{1,0:T(8,128)(2,1)} %refs_16_.4), channel_id=1, source_target_pairs={{0,16},{16,0},{1,17},{17,1},{2,18},{18,2},{3,19},{19,3},{4,20},{20... | collective-permute-start | bytes 3145736 | tf_op jit(solution)/shard_map/ppermute | solution.py:26
  18.0 80.1 %copy-start.4 = (bf16[64,8192]{1,0:T(8,128)(2,1)}, bf16[64,8192]{1,0:T(8,128)(2,1)S(1)}, u32[]{:S(2)}) copy-start(bf16[64,8192]{1,0:T(8,128)(2,1)S(1)} %collective-permute-done.1.refs_2_) | copy-start | bytes 3145732
  18.0 36.2 %collective-permute-start.28 = (bf16[1024,512]{1,0:T(8,128)(2,1)}, bf16[1024,512]{1,0:T(8,128)(2,1)S(1)}, u32[]{:S(2)}, u32[]{:S(2)}) collective-permute-start(bf16[1024,512]{1,0:T(8,128)(2,1)} %refs_16_.7), channel_id=1, source_target_pairs={{0,1},{1,0},{2,3},{3,2},{4,5},{5,4},{6,7},{7,6},{8,9},{9,8},{10,11... | collective-permute-start | bytes 3145736 | tf_op jit(solution)/shard_map/ppermute | solution.py:26
  32.6 74.6 %copy-start = (bf16[64,8192]{1,0:T(8,128)(2,1)}, bf16[64,8192]{1,0:T(8,128)(2,1)S(1)}, u32[]{:S(2)}) copy-start(bf16[64,8192]{1,0:T(8,128)(2,1)S(1)} %collective-permute-done.7.refs_0_.refs_8_) | copy-start | bytes 3145732
  32.6 23.4 %collective-permute-start.2 = (bf16[64,8192]{1,0:T(8,128)(2,1)S(1)}, bf16[64,8192]{1,0:T(8,128)(2,1)S(1)}, u32[]{:S(2)}, u32[]{:S(2)}) collective-permute-start(bf16[64,8192]{1,0:T(8,128)(2,1)S(1)} %collective-permute-done.refs_1_), channel_id=1, source_target_pairs={{0,2},{1,7},{2,4},{3,1},{4,6},{5,3},{6,0},{7,5},{8,10},{9,15},{10,... | collective-permute-start | bytes 3145736 | tf_op jit(solution)/shard_map/ppermute | solution.py:35
  32.6 65.5 %copy-start.9 = (bf16[1024,512]{1,0:T(8,128)(2,1)}, bf16[1024,512]{1,0:T(8,128)(2,1)S(1)}, u32[]{:S(2)}) copy-start(bf16[1024,512]{1,0:T(8,128)(2,1)S(1)} %collective-permute-done.15.refs_9_.refs_7_.refs_17_) | copy-start | bytes 3145732
  32.6 26.1 %collective-permute-start.3 = (bf16[64,8192]{1,0:T(8,128)(2,1)S(1)}, bf16[64,8192]{1,0:T(8,128)(2,1)S(1)}, u32[]{:S(2)}, u32[]{:S(2)}) collective-permute-start(bf16[64,8192]{1,0:T(8,128)(2,1)S(1)} %collective-permute-done.1.refs_2_), channel_id=1, source_target_pairs={{0,1},{1,0},{2,3},{3,2},{4,5},{5,4},{6,7},{7,6},{8,9},{9,8},{10,11... | collective-permute-start | bytes 3145736 | tf_op jit(solution)/shard_map/ppermute | solution.py:26
  33.9 25.3 %collective-permute-start.5 = (bf16[64,8192]{1,0:T(8,128)(2,1)S(1)}, bf16[64,8192]{1,0:T(8,128)(2,1)}, u32[]{:S(2)}, u32[]{:S(2)}) collective-permute-start(bf16[64,8192]{1,0:T(8,128)(2,1)S(1)} %collective-permute-done.1.refs_2_), channel_id=1, source_target_pairs={{0,2},{1,7},{2,4},{3,1},{4,6},{5,3},{6,0},{7,5},{8,10},{9,15},{10,... | collective-permute-start | bytes 3145736 | tf_op jit(solution)/shard_map/ppermute | solution.py:35
  54.2 43.9 %copy-start.11 = (bf16[1024,512]{1,0:T(8,128)(2,1)}, bf16[1024,512]{1,0:T(8,128)(2,1)S(1)}, u32[]{:S(2)}) copy-start(bf16[1024,512]{1,0:T(8,128)(2,1)S(1)} %collective-permute-done.20.refs_20_) | copy-start | bytes 3145732
  54.2 4.9 %collective-permute-start.8 = (bf16[64,8192]{1,0:T(8,128)(2,1)S(1)}, bf16[64,8192]{1,0:T(8,128)(2,1)S(1)}, u32[]{:S(2)}, u32[]{:S(2)}) collective-permute-start(bf16[64,8192]{1,0:T(8,128)(2,1)S(1)} %collective-permute-done.7.refs_0_.refs_8_), channel_id=1, source_target_pairs={{0,1},{1,0},{2,3},{3,2},{4,5},{5,4},{6,7},{7,6},{8,9},{9,8},{10,11... | collective-permute-start | bytes 3145736 | tf_op jit(solution)/shard_map/ppermute | solution.py:26
  54.2 14.7 %collective-permute-start.9 = (bf16[64,8192]{1,0:T(8,128)(2,1)S(1)}, bf16[64,8192]{1,0:T(8,128)(2,1)S(1)}, u32[]{:S(2)}, u32[]{:S(2)}) collective-permute-start(bf16[64,8192]{1,0:T(8,128)(2,1)S(1)} %collective-permute-done.7.refs_0_.refs_8_), channel_id=1, source_target_pairs={{0,2},{1,7},{2,4},{3,1},{4,6},{5,3},{6,0},{7,5},{8,10},{9,15},{10,... | collective-permute-start | bytes 3145736 | tf_op jit(solution)/shard_map/ppermute | solution.py:35
  55.9 42.2 %copy-start.5 = (bf16[64,8192]{1,0:T(8,128)(2,1)}, bf16[64,8192]{1,0:T(8,128)(2,1)S(1)}, u32[]{:S(2)}) copy-start(bf16[64,8192]{1,0:T(8,128)(2,1)S(1)} %collective-permute-done.2.refs_3_) | copy-start | bytes 3145732
  55.9 15.2 %collective-permute-start.17 = (bf16[1024,512]{1,0:T(8,128)(2,1)S(1)}, bf16[1024,512]{1,0:T(8,128)(2,1)S(1)}, u32[]{:S(2)}, u32[]{:S(2)}) collective-permute-start(bf16[1024,512]{1,0:T(8,128)(2,1)S(1)} %collective-permute-done.16), channel_id=1, source_target_pairs={{0,32},{1,97},{32,64},{33,1},{64,96},{65,33},{96,0},{97,65},{2,34}... | collective-permute-start | bytes 3145736 | tf_op jit(solution)/shard_map/ppermute | solution.py:35
  58.7 39.4 %copy-start.6 = (bf16[64,8192]{1,0:T(8,128)(2,1)}, bf16[64,8192]{1,0:T(8,128)(2,1)S(1)}, u32[]{:S(2)}) copy-start(bf16[64,8192]{1,0:T(8,128)(2,1)S(1)} %collective-permute-done.3.refs_4_) | copy-start | bytes 3145732
  58.7 23.0 %collective-permute-start.19 = (bf16[1024,512]{1,0:T(8,128)(2,1)S(1)}, bf16[1024,512]{1,0:T(8,128)(2,1)S(1)}, u32[]{:S(2)}, u32[]{:S(2)}) collective-permute-start(bf16[1024,512]{1,0:T(8,128)(2,1)S(1)} %collective-permute-done.15.refs_9_.refs_7_.refs_17_), channel_id=1, source_target_pairs={{0,32},{1,97},{32,64},{33,1},{64,96},{65,33},{96,0},{97,65},{2,34}... | collective-permute-start | bytes 3145736 | tf_op jit(solution)/shard_map/ppermute | solution.py:35
  59.2 22.9 %collective-permute-start.22 = (bf16[1024,512]{1,0:T(8,128)(2,1)S(1)}, bf16[1024,512]{1,0:T(8,128)(2,1)}, u32[]{:S(2)}, u32[]{:S(2)}) collective-permute-start(bf16[1024,512]{1,0:T(8,128)(2,1)S(1)} %collective-permute-done.20.refs_20_), channel_id=1, source_target_pairs={{0,1},{1,0},{2,3},{3,2},{4,5},{5,4},{6,7},{7,6},{8,9},{9,8},{10,11... | collective-permute-start | bytes 3145736 | tf_op jit(solution)/shard_map/ppermute | solution.py:26
  59.2 48.0 %copy-start.1 = (bf16[64,8192]{1,0:T(8,128)(2,1)}, bf16[64,8192]{1,0:T(8,128)(2,1)S(1)}, u32[]{:S(2)}) copy-start(bf16[64,8192]{1,0:T(8,128)(2,1)S(1)} %collective-permute-done.8.refs_1_.refs_9_) | copy-start | bytes 3145732
  59.2 23.0 %collective-permute-start.4 = (bf16[64,8192]{1,0:T(8,128)(2,1)S(1)}, bf16[64,8192]{1,0:T(8,128)(2,1)S(1)}, u32[]{:S(2)}, u32[]{:S(2)}) collective-permute-start(bf16[64,8192]{1,0:T(8,128)(2,1)S(1)} %collective-permute-done.2.refs_3_), channel_id=1, source_target_pairs={{0,1},{1,0},{2,3},{3,2},{4,5},{5,4},{6,7},{7,6},{8,9},{9,8},{10,11... | collective-permute-start | bytes 3145736 | tf_op jit(solution)/shard_map/ppermute | solution.py:26
  69.0 38.2 %copy-start.2 = (bf16[64,8192]{1,0:T(8,128)(2,1)}, bf16[64,8192]{1,0:T(8,128)(2,1)S(1)}, u32[]{:S(2)}) copy-start(bf16[64,8192]{1,0:T(8,128)(2,1)S(1)} %collective-permute-done.9.refs_2_.refs_10_) | copy-start | bytes 3145732
  69.0 16.7 %collective-permute-start.10 = (bf16[64,8192]{1,0:T(8,128)(2,1)S(1)}, bf16[64,8192]{1,0:T(8,128)(2,1)}, u32[]{:S(2)}, u32[]{:S(2)}) collective-permute-start(bf16[64,8192]{1,0:T(8,128)(2,1)S(1)} %collective-permute-done.8.refs_1_.refs_9_), channel_id=1, source_target_pairs={{0,2},{1,7},{2,4},{3,1},{4,6},{5,3},{6,0},{7,5},{8,10},{9,15},{10,... | collective-permute-start | bytes 3145736 | tf_op jit(solution)/shard_map/ppermute | solution.py:35
  71.1 27.0 %copy-start.16 = (bf16[1024,512]{1,0:T(8,128)(2,1)}, bf16[1024,512]{1,0:T(8,128)(2,1)S(1)}, u32[]{:S(2)}) copy-start(bf16[1024,512]{1,0:T(8,128)(2,1)S(1)} %collective-permute-done.17) | copy-start | bytes 3145732
  71.1 23.2 %collective-permute-start.13 = (bf16[64,8192]{1,0:T(8,128)(2,1)S(1)}, bf16[64,8192]{1,0:T(8,128)(2,1)}, u32[]{:S(2)}, u32[]{:S(2)}) collective-permute-start(bf16[64,8192]{1,0:T(8,128)(2,1)S(1)} %collective-permute-done.9.refs_2_.refs_10_), channel_id=1, source_target_pairs={{0,2},{1,7},{2,4},{3,1},{4,6},{5,3},{6,0},{7,5},{8,10},{9,15},{10,... | collective-permute-start | bytes 3145736 | tf_op jit(solution)/shard_map/ppermute | solution.py:35
  81.7 16.5 %collective-permute-start.6 = (bf16[64,8192]{1,0:T(8,128)(2,1)}, bf16[64,8192]{1,0:T(8,128)(2,1)}, u32[]{:S(2)}, u32[]{:S(2)}) collective-permute-start(bf16[64,8192]{1,0:T(8,128)(2,1)} %collective-permute-done.5.refs_6_), channel_id=1, source_target_pairs={{0,1},{1,0},{2,3},{3,2},{4,5},{5,4},{6,7},{7,6},{8,9},{9,8},{10,11... | collective-permute-start | bytes 3145736 | tf_op jit(solution)/shard_map/ppermute | solution.py:26
  82.1 19.9 %collective-permute-start.11 = (bf16[64,8192]{1,0:T(8,128)(2,1)S(1)}, bf16[64,8192]{1,0:T(8,128)(2,1)}, u32[]{:S(2)}, u32[]{:S(2)}) collective-permute-start(bf16[64,8192]{1,0:T(8,128)(2,1)S(1)} %collective-permute-done.9.refs_2_.refs_10_), channel_id=1, source_target_pairs={{0,1},{1,0},{2,3},{3,2},{4,5},{5,4},{6,7},{7,6},{8,9},{9,8},{10,11... | collective-permute-start | bytes 3145736 | tf_op jit(solution)/shard_map/ppermute | solution.py:26
  82.2 22.5 %collective-permute-start.23 = (bf16[1024,512]{1,0:T(8,128)(2,1)}, bf16[1024,512]{1,0:T(8,128)(2,1)}, u32[]{:S(2)}, u32[]{:S(2)}) collective-permute-start(bf16[1024,512]{1,0:T(8,128)(2,1)} %collective-permute-done.22), channel_id=1, source_target_pairs={{0,32},{1,97},{32,64},{33,1},{64,96},{65,33},{96,0},{97,65},{2,34}... | collective-permute-start | bytes 3145736 | tf_op jit(solution)/shard_map/ppermute | solution.py:35
  85.7 20.2 %collective-permute-start.12 = (bf16[64,8192]{1,0:T(8,128)(2,1)}, bf16[64,8192]{1,0:T(8,128)(2,1)}, u32[]{:S(2)}, u32[]{:S(2)}) collective-permute-start(bf16[64,8192]{1,0:T(8,128)(2,1)} %collective-permute-done.10.refs_3_.refs_11_), channel_id=1, source_target_pairs={{0,1},{1,0},{2,3},{3,2},{4,5},{5,4},{6,7},{7,6},{8,9},{9,8},{10,11... | collective-permute-start | bytes 3145736 | tf_op jit(solution)/shard_map/ppermute | solution.py:26
  94.3 12.9 %collective-permute-start.14 = (bf16[64,8192]{1,0:T(8,128)(2,1)}, bf16[64,8192]{1,0:T(8,128)(2,1)}, u32[]{:S(2)}, u32[]{:S(2)}) collective-permute-start(bf16[64,8192]{1,0:T(8,128)(2,1)} %collective-permute-done.13.refs_14_), channel_id=1, source_target_pairs={{0,1},{1,0},{2,3},{3,2},{4,5},{5,4},{6,7},{7,6},{8,9},{9,8},{10,11... | collective-permute-start | bytes 3145736 | tf_op jit(solution)/shard_map/ppermute | solution.py:26
  98.2 18.1 %collective-permute-start.18 = (bf16[1024,512]{1,0:T(8,128)(2,1)}, bf16[1024,512]{1,0:T(8,128)(2,1)}, u32[]{:S(2)}, u32[]{:S(2)}) collective-permute-start(bf16[1024,512]{1,0:T(8,128)(2,1)} %copy-done.16), channel_id=1, source_target_pairs={{0,1},{1,0},{2,3},{3,2},{4,5},{5,4},{6,7},{7,6},{8,9},{9,8},{10,11... | collective-permute-start | bytes 3145736 | tf_op jit(solution)/shard_map/ppermute | solution.py:26
  102.0 34.1 %collective-permute-start.21 = (bf16[1024,512]{1,0:T(8,128)(2,1)}, bf16[1024,512]{1,0:T(8,128)(2,1)}, u32[]{:S(2)}, u32[]{:S(2)}) collective-permute-start(bf16[1024,512]{1,0:T(8,128)(2,1)} %copy-done.11), channel_id=1, source_target_pairs={{0,32},{1,97},{32,64},{33,1},{64,96},{65,33},{96,0},{97,65},{2,34}... | collective-permute-start | bytes 3145736 | tf_op jit(solution)/shard_map/ppermute | solution.py:35
  104.7 32.9 %collective-permute-start.25 = (bf16[1024,512]{1,0:T(8,128)(2,1)}, bf16[1024,512]{1,0:T(8,128)(2,1)}, u32[]{:S(2)}, u32[]{:S(2)}) collective-permute-start(bf16[1024,512]{1,0:T(8,128)(2,1)} %copy-done.10), channel_id=1, source_target_pairs={{0,16},{16,0},{1,17},{17,1},{2,18},{18,2},{3,19},{19,3},{4,20},{20... | collective-permute-start | bytes 3145736 | tf_op jit(solution)/shard_map/ppermute | solution.py:26
  105.9 32.2 %collective-permute-start.24 = (bf16[1024,512]{1,0:T(8,128)(2,1)}, bf16[1024,512]{1,0:T(8,128)(2,1)}, u32[]{:S(2)}, u32[]{:S(2)}) collective-permute-start(bf16[1024,512]{1,0:T(8,128)(2,1)} %collective-permute-done.23), channel_id=1, source_target_pairs={{0,1},{1,0},{2,3},{3,2},{4,5},{5,4},{6,7},{7,6},{8,9},{9,8},{10,11... | collective-permute-start | bytes 3145736 | tf_op jit(solution)/shard_map/ppermute | solution.py:26
  114.3 34.8 %collective-permute-start.32 = (bf16[1024,512]{1,0:T(8,128)(2,1)}, bf16[1024,512]{1,0:T(8,128)(2,1)}, u32[]{:S(2)}, u32[]{:S(2)}) collective-permute-start(bf16[1024,512]{1,0:T(8,128)(2,1)} %get-tuple-element.28), channel_id=1, source_target_pairs={{0,32},{1,97},{32,64},{33,1},{64,96},{65,33},{96,0},{97,65},{2,34}... | collective-permute-start | bytes 3145736 | tf_op jit(solution)/shard_map/ppermute | solution.py:35
  122.8 36.1 %collective-permute-start.35 = (bf16[1024,512]{1,0:T(8,128)(2,1)S(1)}, bf16[1024,512]{1,0:T(8,128)(2,1)S(1)}, u32[]{:S(2)}, u32[]{:S(2)}) collective-permute-start(bf16[1024,512]{1,0:T(8,128)(2,1)S(1)} %copy-done.17), channel_id=1, source_target_pairs={{0,16},{16,0},{1,17},{17,1},{2,18},{18,2},{3,19},{19,3},{4,20},{20... | collective-permute-start | bytes 3145736 | tf_op jit(solution)/shard_map/ppermute | solution.py:26
  136.1 42.9 %collective-permute-start.31 = (bf16[1024,512]{1,0:T(8,128)(2,1)}, bf16[1024,512]{1,0:T(8,128)(2,1)}, u32[]{:S(2)}, u32[]{:S(2)}) collective-permute-start(bf16[1024,512]{1,0:T(8,128)(2,1)} %get-tuple-element.27), channel_id=1, source_target_pairs={{0,32},{1,97},{32,64},{33,1},{64,96},{65,33},{96,0},{97,65},{2,34}... | collective-permute-start | bytes 3145736 | tf_op jit(solution)/shard_map/ppermute | solution.py:35
  137.7 40.8 %collective-permute-start.29 = (bf16[1024,512]{1,0:T(8,128)(2,1)}, bf16[1024,512]{1,0:T(8,128)(2,1)}, u32[]{:S(2)}, u32[]{:S(2)}) collective-permute-start(bf16[1024,512]{1,0:T(8,128)(2,1)} %get-tuple-element.25), channel_id=1, source_target_pairs={{0,32},{1,97},{32,64},{33,1},{64,96},{65,33},{96,0},{97,65},{2,34}... | collective-permute-start | bytes 3145736 | tf_op jit(solution)/shard_map/ppermute | solution.py:35
  149.2 29.8 %collective-permute-start.33 = (bf16[1024,512]{1,0:T(8,128)(2,1)}, bf16[1024,512]{1,0:T(8,128)(2,1)}, u32[]{:S(2)}, u32[]{:S(2)}) collective-permute-start(bf16[1024,512]{1,0:T(8,128)(2,1)} %collective-permute-done.32), channel_id=1, source_target_pairs={{0,1},{1,0},{2,3},{3,2},{4,5},{5,4},{6,7},{7,6},{8,9},{9,8},{10,11... | collective-permute-start | bytes 3145736 | tf_op jit(solution)/shard_map/ppermute | solution.py:26
  160.4 22.8 %collective-permute-start.36 = (bf16[1024,512]{1,0:T(8,128)(2,1)S(1)}, bf16[1024,512]{1,0:T(8,128)(2,1)}, u32[]{:S(2)}, u32[]{:S(2)}) collective-permute-start(bf16[1024,512]{1,0:T(8,128)(2,1)S(1)} %add_convert_fusion.2), channel_id=1, source_target_pairs={{0,32},{1,97},{32,64},{33,1},{64,96},{65,33},{96,0},{97,65},{2,34}... | collective-permute-start | bytes 3145736 | tf_op jit(solution)/shard_map/ppermute | solution.py:35
  178.4 4.8 %collective-permute-start.26 = (bf16[128,1024]{1,0:T(8,128)(2,1)}, bf16[128,1024]{1,0:T(8,128)(2,1)S(1)}, u32[]{:S(2)}, u32[]{:S(2)}) collective-permute-start(bf16[128,1024]{1,0:T(8,128)(2,1)} %get-tuple-element.23), channel_id=1, source_target_pairs={{0,1},{1,0},{2,3},{3,2},{4,5},{5,4},{6,7},{7,6},{8,9},{9,8},{10,11... | collective-permute-start | bytes 786440 | tf_op jit(solution)/shard_map/ppermute | solution.py:26
  178.5 13.6 %collective-permute-start.30 = (bf16[1024,512]{1,0:T(8,128)(2,1)}, bf16[1024,512]{1,0:T(8,128)(2,1)S(1)}, u32[]{:S(2)}, u32[]{:S(2)}) collective-permute-start(bf16[1024,512]{1,0:T(8,128)(2,1)} %collective-permute-done.29), channel_id=1, source_target_pairs={{0,1},{1,0},{2,3},{3,2},{4,5},{5,4},{6,7},{7,6},{8,9},{9,8},{10,11... | collective-permute-start | bytes 3145736 | tf_op jit(solution)/shard_map/ppermute | solution.py:26
  182.0 24.9 %collective-permute-start.34 = (bf16[1024,512]{1,0:T(8,128)(2,1)}, bf16[1024,512]{1,0:T(8,128)(2,1)}, u32[]{:S(2)}, u32[]{:S(2)}) collective-permute-start(bf16[1024,512]{1,0:T(8,128)(2,1)} %add_convert_fusion.3), channel_id=1, source_target_pairs={{0,16},{16,0},{1,17},{17,1},{2,18},{18,2},{3,19},{19,3},{4,20},{20... | collective-permute-start | bytes 3145736 | tf_op jit(solution)/shard_map/ppermute | solution.py:26
  185.9 22.7 %collective-permute-start.37 = (bf16[1024,512]{1,0:T(8,128)(2,1)}, bf16[1024,512]{1,0:T(8,128)(2,1)}, u32[]{:S(2)}, u32[]{:S(2)}) collective-permute-start(bf16[1024,512]{1,0:T(8,128)(2,1)} %add_convert_fusion.1), channel_id=1, source_target_pairs={{0,32},{1,97},{32,64},{33,1},{64,96},{65,33},{96,0},{97,65},{2,34}... | collective-permute-start | bytes 3145736 | tf_op jit(solution)/shard_map/ppermute | solution.py:35
  186.4 5.0 %collective-permute-start.27 = (bf16[2,32,1024]{2,1,0:T(8,128)(2,1)S(1)}, bf16[2,32,1024]{2,1,0:T(8,128)(2,1)S(1)}, u32[]{:S(2)}, u32[]{:S(2)}) collective-permute-start(bf16[2,32,1024]{2,1,0:T(8,128)(2,1)S(1)} %fusion.1), channel_id=1, source_target_pairs={{0,2},{2,0},{4,6},{6,4},{1,3},{3,1},{5,7},{7,5},{8,10},{10,8},{12,... | collective-permute-start | bytes 393224 | tf_op jit(solution)/shard_map/ppermute | solution.py:419
  (8 other events, 84.8 us)

commit v3 on v2

--- a/solution.py
+++ b/solution.py
@@ -382,10 +382,8 @@
         return terms(order, dest, side, pieces, attended, attended_other)
 
     other_p, far_p = call(dests([0, 2], [1, 0], [1, 1]), [1, 0])
-    near_p, other_o = call(dests([0, 0], [1, 1], [1, 0]), [0, 1])
-    far_o, near_o, own_p, own_o = call(
-        dests([2, 0, 0, 0], [0, 1, 0, 0], [0, 0, 1, 0]), [0, 0, 0, 0]
-    )
+    near_p, other_o, far_o = call(dests([0, 0, 2], [1, 1, 0], [1, 0, 0]), [0, 1, 0])
+    near_o, own_p, own_o = call(dests([0, 0, 0], [1, 0, 0], [0, 1, 0]), [0, 0, 0])
     far = added(far_o, swap(far_p, "xl"))
     far = along(far, "y")
     near_p = along(near_p, "y")

time: 212 us -> 209 us (0.986)
  other arithmetic: 17.1 us -> 13.8 us
    convert_element_type x4, other arithmetic: 9.74 us -> 6.25 us  [added(): return total.astype(jnp.bfloat16)]
  transfers between devices with their start and end apart: 38 -> 38, of which waited for: 8 -> 8; matrix products, arithmetic and copies ran while one was open for 7% -> 6% of each run, Pallas kernels for 29% -> 30%
where the time goes in v3:
time: 209 us
  waiting for transfers between devices  88 us (42%)
  Pallas kernels  62.1 us (30%)
  starting transfers between devices  43.5 us (21%)
  other arithmetic  13.8 us (7%)
    ppermute x21, waiting for transfers between devices, swap(): return lax.ppermute(x, axis, [(0, 1), (1, 0)])  49.9 us
    ppermute x16, waiting for transfers between devices, along(): return lax.ppermute(x, (axis, 'c'), pairs)  33.3 us
    ppermute x16, starting transfers between devices, along(): return lax.ppermute(x, (axis, 'c'), pairs)  26.7 us
    pallas_call x3, Pallas kernels, terms(): pl.pallas_call(functools.partial(terms_kernel, side=side), in_specs=[smal...  23.6 us
    pallas_call x3, Pallas kernels, partial_dot(): pl.pallas_call(kernel, in_specs=[small] * 2 + [large] * (len(pieces) + le...  23.3 us
    ppermute x21, starting transfers between devices, swap(): return lax.ppermute(x, axis, [(0, 1), (1, 0)])  16.7 us
    pallas_call x2, Pallas kernels, call(): pl.pallas_call(functools.partial(head_kernel, first=first, count=count),...  15.2 us
    convert_element_type x4, other arithmetic, added(): return total.astype(jnp.bfloat16)  6.25 us
  transfers between devices with their start and end apart: 38, of which 8 were waited for; matrix products, arithmetic and copies ran while one was open for 6% of the time, Pallas kernels for 30%

profile of v3, /device:TPU:1, one launch (start us, length us, event | category | flops | bytes accessed | tf_op | source)
XLA Modules:
  0.0 209.1 jit_solution(12796527429435872398)
XLA Ops:
  0.6 1.5 collective-permute-start
  2.1 3.9 %collective-permute-start.1 = (bf16[64,8192]{1,0:T(8,128)(2,1)}, bf16[64,8192]{1,0:T(8,128)(2,1)S(1)}, u32[]{:S(2)}, u32[]{:S(2)}) collective-permute-start(bf16[64,8192]{1,0:T(8,128)(2,1)} %refs_0_.13), channel_id=1, source_target_pairs={{0,2},{1,7},{2,4},{3,1},{4,6},{5,3},{6,0},{7,5},{8,10},{9,15},{10,... | collective-permute-start | bytes 3145736 | tf_op jit(solution)/shard_map/ppermute | solution.py:35
  6.0 2.7 %collective-permute-start.7 = (bf16[64,8192]{1,0:T(8,128)(2,1)}, bf16[64,8192]{1,0:T(8,128)(2,1)S(1)}, u32[]{:S(2)}, u32[]{:S(2)}) collective-permute-start(bf16[64,8192]{1,0:T(8,128)(2,1)} %refs_0_.13), channel_id=1, source_target_pairs={{0,8},{8,0},{1,9},{9,1},{2,10},{10,2},{3,11},{11,3},{4,12},{12,4},... | collective-permute-start | bytes 3145736 | tf_op jit(solution)/shard_map/ppermute | solution.py:26
  8.7 2.7 %collective-permute-start.15 = (bf16[1024,512]{1,0:T(8,128)(2,1)}, bf16[1024,512]{1,0:T(8,128)(2,1)S(1)}, u32[]{:S(2)}, u32[]{:S(2)}) collective-permute-start(bf16[1024,512]{1,0:T(8,128)(2,1)} %refs_16_.4), channel_id=1, source_target_pairs={{0,32},{1,97},{32,64},{33,1},{64,96},{65,33},{96,0},{97,65},{2,34}... | collective-permute-start | bytes 3145736 | tf_op jit(solution)/shard_map/ppermute | solution.py:35
  11.8 6.2 %collective-permute-done.1.refs_2_ = bf16[64,8192]{1,0:T(8,128)(2,1)S(1)} collective-permute-done((bf16[64,8192]{1,0:T(8,128)(2,1)}, bf16[64,8192]{1,0:T(8,128)(2,1)S(1)}, u32[]{:S(2)}, u32[]{:S(2)}) %collective-permute-start.1) | collective-permute-done | bytes 1048608 | tf_op jit(solution)/shard_map/ppermute | solution.py:35
  18.0 1.3 collective-permute-start.28
  19.3 13.2 %collective-permute-done.7.refs_0_.refs_8_ = bf16[64,8192]{1,0:T(8,128)(2,1)S(1)} collective-permute-done((bf16[64,8192]{1,0:T(8,128)(2,1)}, bf16[64,8192]{1,0:T(8,128)(2,1)S(1)}, u32[]{:S(2)}, u32[]{:S(2)}) %collective-permute-start.7) | collective-permute-done | bytes 1048608 | tf_op jit(solution)/shard_map/ppermute | solution.py:26
  32.6 1.3 collective-permute-start.3
  34.0 20.2 %collective-permute-done.20.refs_20_ = bf16[1024,512]{1,0:T(8,128)(2,1)S(1)} collective-permute-done((bf16[1024,512]{1,0:T(8,128)(2,1)}, bf16[1024,512]{1,0:T(8,128)(2,1)S(1)}, u32[]{:S(2)}, u32[]{:S(2)}) %collective-permute-start.20) | collective-permute-done | bytes 1048608 | tf_op jit(solution)/shard_map/ppermute | solution.py:26
  54.2 1.7 collective-permute-start.9
  55.9 2.7 %collective-permute-start.17 = (bf16[1024,512]{1,0:T(8,128)(2,1)S(1)}, bf16[1024,512]{1,0:T(8,128)(2,1)S(1)}, u32[]{:S(2)}, u32[]{:S(2)}) collective-permute-start(bf16[1024,512]{1,0:T(8,128)(2,1)S(1)} %collective-permute-done.16), channel_id=1, source_target_pairs={{0,32},{1,97},{32,64},{33,1},{64,96},{65,33},{96,0},{97,65},{2,34}... | collective-permute-start | bytes 3145736 | tf_op jit(solution)/shard_map/ppermute | solution.py:35
  58.7 0.5 collective-permute-start.19
  59.2 0.6 collective-permute-start.4
  59.7 9.2 %collective-permute-done.9.refs_2_.refs_10_ = bf16[64,8192]{1,0:T(8,128)(2,1)S(1)} collective-permute-done((bf16[64,8192]{1,0:T(8,128)(2,1)S(1)}, bf16[64,8192]{1,0:T(8,128)(2,1)S(1)}, u32[]{:S(2)}, u32[]{:S(2)}) %collective-permute-start.9) | collective-permute-done | bytes 1048608 | tf_op jit(solution)/shard_map/ppermute | solution.py:35
  69.0 2.1 %collective-permute-start.10 = (bf16[64,8192]{1,0:T(8,128)(2,1)S(1)}, bf16[64,8192]{1,0:T(8,128)(2,1)}, u32[]{:S(2)}, u32[]{:S(2)}) collective-permute-start(bf16[64,8192]{1,0:T(8,128)(2,1)S(1)} %collective-permute-done.8.refs_1_.refs_9_), channel_id=1, source_target_pairs={{0,2},{1,7},{2,4},{3,1},{4,6},{5,3},{6,0},{7,5},{8,10},{9,15},{10,... | collective-permute-start | bytes 3145736 | tf_op jit(solution)/shard_map/ppermute | solution.py:35
  71.2 10.5 %collective-permute-done.19.refs_11_.refs_9_.refs_19_ = bf16[1024,512]{1,0:T(8,128)(2,1)S(1)} collective-permute-done((bf16[1024,512]{1,0:T(8,128)(2,1)S(1)}, bf16[1024,512]{1,0:T(8,128)(2,1)S(1)}, u32[]{:S(2)}, u32[]{:S(2)}) %collective-permute-start.19) | collective-permute-done | bytes 1048608 | tf_op jit(solution)/shard_map/ppermute | solution.py:35
  82.2 3.5 %collective-permute-start.23 = (bf16[1024,512]{1,0:T(8,128)(2,1)}, bf16[1024,512]{1,0:T(8,128)(2,1)}, u32[]{:S(2)}, u32[]{:S(2)}) collective-permute-start(bf16[1024,512]{1,0:T(8,128)(2,1)} %collective-permute-done.22), channel_id=1, source_target_pairs={{0,32},{1,97},{32,64},{33,1},{64,96},{65,33},{96,0},{97,65},{2,34}... | collective-permute-start | bytes 3145736 | tf_op jit(solution)/shard_map/ppermute | solution.py:35
  85.7 1.2 collective-permute-start.12
  86.9 7.4 %collective-permute-done.13.refs_14_ = bf16[64,8192]{1,0:T(8,128)(2,1)} collective-permute-done((bf16[64,8192]{1,0:T(8,128)(2,1)S(1)}, bf16[64,8192]{1,0:T(8,128)(2,1)}, u32[]{:S(2)}, u32[]{:S(2)}) %collective-permute-start.13) | collective-permute-done | bytes 1048608 | tf_op jit(solution)/shard_map/ppermute | solution.py:35
  94.3 3.8 %collective-permute-start.14 = (bf16[64,8192]{1,0:T(8,128)(2,1)}, bf16[64,8192]{1,0:T(8,128)(2,1)}, u32[]{:S(2)}, u32[]{:S(2)}) collective-permute-start(bf16[64,8192]{1,0:T(8,128)(2,1)} %collective-permute-done.13.refs_14_), channel_id=1, source_target_pairs={{0,1},{1,0},{2,3},{3,2},{4,5},{5,4},{6,7},{7,6},{8,9},{9,8},{10,11... | collective-permute-start | bytes 3145736 | tf_op jit(solution)/shard_map/ppermute | solution.py:26
  98.2 0.6 pad_add_fusion.where
  98.8 1.2 fusion.3.place
  100.0 1.2 fusion.2.order
  101.2 1.3 fusion.4
  102.5 2.7 %collective-permute-start.21 = (bf16[1024,512]{1,0:T(8,128)(2,1)}, bf16[1024,512]{1,0:T(8,128)(2,1)}, u32[]{:S(2)}, u32[]{:S(2)}) collective-permute-start(bf16[1024,512]{1,0:T(8,128)(2,1)} %copy-done.11), channel_id=1, source_target_pairs={{0,32},{1,97},{32,64},{33,1},{64,96},{65,33},{96,0},{97,65},{2,34}... | collective-permute-start | bytes 3145736 | tf_op jit(solution)/shard_map/ppermute | solution.py:35
  105.2 1.2 collective-permute-start.25
  106.4 1.2 fusion.18.dest
  107.6 7.1 %shard_map.235 = (bf16[1024,512]{1,0:T(8,128)(2,1)}, bf16[1024,512]{1,0:T(8,128)(2,1)}) custom-call(s32[16]{0:T(128)} %fusion.2.order, s32[2]{0:T(128)} %fusion.18.dest, bf16[64,8192]{1,0:T(8,128)(2,1)} %refs_0_.13, bf16[64,8192]{1,0:T(8,128)(2,1)} %copy-done.3, bf16[64,8192]{1,0:T(8,128)(2,1)} %copy-done.4, bf16[64,8192]{1,0:T(8,128)(2,1)} %copy-done.5, ...), custom_call_target="tpu_custom_call" | custom-call | flops 2147483648 | bytes 6291456 | tf_op jit(solution)/shard_map/pallas_call | solution.py:140
  114.7 1.2 collective-permute-start.32
  116.0 6.4 %shard_map.228.refs_24_ = f32[512,512]{1,0:T(8,128)} custom-call(s32[16]{0:T(128)} %fusion.2.order, s32[8]{0:T(128)} %fusion.3.place, bf16[64,8192]{1,0:T(8,128)(2,1)} %refs_0_.13, bf16[64,8192]{1,0:T(8,128)(2,1)} %copy-done.3, bf16[64,8192]{1,0:T(8,128)(2,1)} %copy-done.4, bf16[64,8192]{1,0:T(8,128)(2,1)} %copy-done.5, bf16[64,8192]{1,0:T(8,128)(2,1)} %copy-done.6, ...), custom_call_target="tpu_custom_call" | custom-call | flops 2147483648 | bytes 12582912 | tf_op jit(solution)/shard_map/pallas_call | solution.py:236
  122.8 5.8 %shard_map.229.refs_25_ = f32[384,512]{1,0:T(8,128)} custom-call(s32[16]{0:T(128)} %fusion.2.order, s32[8]{0:T(128)} %fusion.3.place, bf16[64,8192]{1,0:T(8,128)(2,1)} %copy-done, bf16[64,8192]{1,0:T(8,128)(2,1)} %copy-done.1, bf16[64,8192]{1,0:T(8,128)(2,1)} %copy-done.2, bf16[64,8192]{1,0:T(8,128)(2,1)} %collective-permute-done.10.refs_3_.refs_11_, ...), custom_call_target="tpu_custom_call" | custom-call | flops 1610612736 | bytes 12582912 | tf_op jit(solution)/shard_map/pallas_call | solution.py:236
  128.6 8.4 %shard_map.234 = (bf16[1024,512]{1,0:T(8,128)(2,1)}, bf16[1024,512]{1,0:T(8,128)(2,1)}, bf16[1024,512]{1,0:T(8,128)(2,1)}) custom-call(s32[16]{0:T(128)} %fusion.2.order, s32[3]{0:T(128)} %get-tuple-element.35.dest, bf16[64,8192]{1,0:T(8,128)(2,1)} %refs_0_.13, bf16[64,8192]{1,0:T(8,128)(2,1)} %copy-done.3, bf16[64,8192]{1,0:T(8,128)(2,1)} %copy-done.4, ...), custom_call_target="tpu_custom_call" | custom-call | flops 3221225472 | bytes 9437184 | tf_op jit(solution)/shard_map/pallas_call | solution.py:140
  137.0 1.6 collective-permute-start.31
  139.1 11.1 %shard_map.230.refs_3_ = bf16[1024,512]{1,0:T(8,128)(2,1)} custom-call(s32[16]{0:T(128)} %fusion.2.order, s32[8]{0:T(128)} %fusion.3.place, bf16[64,8192]{1,0:T(8,128)(2,1)} %refs_0_.13, bf16[64,8192]{1,0:T(8,128)(2,1)} %copy-done.3, bf16[64,8192]{1,0:T(8,128)(2,1)} %copy-done.4, bf16[64,8192]{1,0:T(8,128)(2,1)} %copy-done.5, bf16[64,8192]{1,0:T(8,128)(2,1)} %copy-done.6, ...), custom_call_target="tpu_custom_call" | custom-call | flops 4831838208 | bytes 25165824 | tf_op jit(solution)/shard_map/pallas_call | solution.py:236
  150.3 7.3 %shard_map.231 = (bf16[1024,512]{1,0:T(8,128)(2,1)}, f32[1024,128]{1,0:T(8,128)}, f32[1024,128]{1,0:T(8,128)}) custom-call(s32[2]{0:T(128)} %pad_add_fusion.where, bf16[1024,512]{1,0:T(8,128)(2,1)} %refs_0_.10, bf16[1024,512]{1,0:T(8,128)(2,1)} %refs_1_.3, bf16[1024,512]{1,0:T(8,128)(2,1)} %refs_2_.3, bf16[1024,512]{1,0:T(8,128)(2,1)} %shard_map.230.refs_3_, ...), custom_call_target="tpu_custom_call" | custom-call | flops 2684354560 | bytes 4194304 | tf_op jit(solution)/shard_map/pallas_call | solution.py:344
  157.9 2.9 %collective-permute-start.36 = (bf16[1024,512]{1,0:T(8,128)(2,1)S(1)}, bf16[1024,512]{1,0:T(8,128)(2,1)S(1)}, u32[]{:S(2)}, u32[]{:S(2)}) collective-permute-start(bf16[1024,512]{1,0:T(8,128)(2,1)S(1)} %add_convert_fusion.2), channel_id=1, source_target_pairs={{0,32},{1,97},{32,64},{33,1},{64,96},{65,33},{96,0},{97,65},{2,34}... | collective-permute-start | bytes 3145736 | tf_op jit(solution)/shard_map/ppermute | solution.py:35
  160.8 7.9 %shard_map.232 = (bf16[1024,512]{1,0:T(8,128)(2,1)}, f32[128,1024]{1,0:T(8,128)}, bf16[128,1024]{1,0:T(8,128)(2,1)}) custom-call(s32[2]{0:T(128)} %pad_add_fusion.where, bf16[1024,512]{1,0:T(8,128)(2,1)} %refs_0_.10, bf16[1024,512]{1,0:T(8,128)(2,1)} %refs_1_.3, bf16[1024,512]{1,0:T(8,128)(2,1)} %refs_2_.3, ...), custom_call_target="tpu_custom_call", output_to_operand_aliasing={{0}: (9, {})} | custom-call | flops 2684354560 | bytes 4194304 | tf_op jit(solution)/shard_map/pallas_call | solution.py:344
  168.8 8.1 %shard_map.233 = (bf16[1024,512]{1,0:T(8,128)(2,1)}, bf16[1024,512]{1,0:T(8,128)(2,1)}, bf16[1024,512]{1,0:T(8,128)(2,1)}) custom-call(s32[16]{0:T(128)} %fusion.2.order, s32[3]{0:T(128)} %get-tuple-element.34.dest, bf16[64,8192]{1,0:T(8,128)(2,1)} %refs_0_.13, bf16[64,8192]{1,0:T(8,128)(2,1)} %copy-done.3, bf16[64,8192]{1,0:T(8,128)(2,1)} %copy-done.4, ...), custom_call_target="tpu_custom_call" | custom-call | flops 3221225472 | bytes 9437184 | tf_op jit(solution)/shard_map/pallas_call | solution.py:140
  176.9 0.6 collective-permute-start.30
  177.5 3.4 %add_convert_fusion.3 = bf16[1024,512]{1,0:T(8,128)(2,1)} fusion(bf16[1024,512]{1,0:T(8,128)(2,1)} %collective-permute-done.33, bf16[1024,512]{1,0:T(8,128)(2,1)} %collective-permute-done.31, bf16[1024,512]{1,0:T(8,128)(2,1)} %get-tuple-element.26), kind=kLoop, calls=%fused_computation.4 | loop fusion | flops 3145728 | bytes 4194304 | tf_op jit(solution)/shard_map/convert_element_type | solution.py:371
  180.8 1.2 collective-permute-start.34
  182.1 1.3 add_convert_fusion.1
  183.4 0.5 collective-permute-start.37
  184.0 4.8 %collective-permute-done.27 = bf16[2,32,1024]{2,1,0:T(8,128)(2,1)S(1)} collective-permute-done((bf16[2,32,1024]{2,1,0:T(8,128)(2,1)S(1)}, bf16[2,32,1024]{2,1,0:T(8,128)(2,1)S(1)}, u32[]{:S(2)}, u32[]{:S(2)}) %collective-permute-start.27) | collective-permute-done | bytes 131104 | tf_op jit(solution)/shard_map/ppermute | solution.py:417
  188.7 0.7 slice_bitcast_fusion
  189.4 16.4 %collective-permute-done.34 = bf16[1024,512]{1,0:T(8,128)(2,1)} collective-permute-done((bf16[1024,512]{1,0:T(8,128)(2,1)}, bf16[1024,512]{1,0:T(8,128)(2,1)}, u32[]{:S(2)}, u32[]{:S(2)}) %collective-permute-start.34) | collective-permute-done | bytes 1048608 | tf_op jit(solution)/shard_map/ppermute | solution.py:26
  205.8 2.0 convert_add_fusion
  207.8 1.3 add_convert_fusion
  (86 shorter events, 2.8 us)
Async XLA Ops:
  0.6 10.8 %collective-permute-start = (bf16[64,8192]{1,0:T(8,128)(2,1)}, bf16[64,8192]{1,0:T(8,128)(2,1)S(1)}, u32[]{:S(2)}, u32[]{:S(2)}) collective-permute-start(bf16[64,8192]{1,0:T(8,128)(2,1)} %refs_0_.13), channel_id=1, source_target_pairs={{0,1},{1,0},{2,3},{3,2},{4,5},{5,4},{6,7},{7,6},{8,9},{9,8},{10,11... | collective-permute-start | bytes 3145736 | tf_op jit(solution)/shard_map/ppermute | solution.py:26
  2.1 15.9 %collective-permute-start.1 = (bf16[64,8192]{1,0:T(8,128)(2,1)}, bf16[64,8192]{1,0:T(8,128)(2,1)S(1)}, u32[]{:S(2)}, u32[]{:S(2)}) collective-permute-start(bf16[64,8192]{1,0:T(8,128)(2,1)} %refs_0_.13), channel_id=1, source_target_pairs={{0,2},{1,7},{2,4},{3,1},{4,6},{5,3},{6,0},{7,5},{8,10},{9,15},{10,... | collective-permute-start | bytes 3145736 | tf_op jit(solution)/shard_map/ppermute | solution.py:35
  6.0 26.6 %collective-permute-start.7 = (bf16[64,8192]{1,0:T(8,128)(2,1)}, bf16[64,8192]{1,0:T(8,128)(2,1)S(1)}, u32[]{:S(2)}, u32[]{:S(2)}) collective-permute-start(bf16[64,8192]{1,0:T(8,128)(2,1)} %refs_0_.13), channel_id=1, source_target_pairs={{0,8},{8,0},{1,9},{9,1},{2,10},{10,2},{3,11},{11,3},{4,12},{12,4},... | collective-permute-start | bytes 3145736 | tf_op jit(solution)/shard_map/ppermute | solution.py:26
  8.7 23.9 %collective-permute-start.15 = (bf16[1024,512]{1,0:T(8,128)(2,1)}, bf16[1024,512]{1,0:T(8,128)(2,1)S(1)}, u32[]{:S(2)}, u32[]{:S(2)}) collective-permute-start(bf16[1024,512]{1,0:T(8,128)(2,1)} %refs_16_.4), channel_id=1, source_target_pairs={{0,32},{1,97},{32,64},{33,1},{64,96},{65,33},{96,0},{97,65},{2,34}... | collective-permute-start | bytes 3145736 | tf_op jit(solution)/shard_map/ppermute | solution.py:35
  11.4 22.4 %collective-permute-start.16 = (bf16[1024,512]{1,0:T(8,128)(2,1)}, bf16[1024,512]{1,0:T(8,128)(2,1)S(1)}, u32[]{:S(2)}, u32[]{:S(2)}) collective-permute-start(bf16[1024,512]{1,0:T(8,128)(2,1)} %refs_16_.4), channel_id=1, source_target_pairs={{0,1},{1,0},{2,3},{3,2},{4,5},{5,4},{6,7},{7,6},{8,9},{9,8},{10,11... | collective-permute-start | bytes 3145736 | tf_op jit(solution)/shard_map/ppermute | solution.py:26
  11.4 82.8 %copy-start.3 = (bf16[64,8192]{1,0:T(8,128)(2,1)}, bf16[64,8192]{1,0:T(8,128)(2,1)S(1)}, u32[]{:S(2)}) copy-start(bf16[64,8192]{1,0:T(8,128)(2,1)S(1)} %collective-permute-done.refs_1_) | copy-start | bytes 3145732
  11.5 42.8 %collective-permute-start.20 = (bf16[1024,512]{1,0:T(8,128)(2,1)}, bf16[1024,512]{1,0:T(8,128)(2,1)S(1)}, u32[]{:S(2)}, u32[]{:S(2)}) collective-permute-start(bf16[1024,512]{1,0:T(8,128)(2,1)} %refs_16_.4), channel_id=1, source_target_pairs={{0,16},{16,0},{1,17},{17,1},{2,18},{18,2},{3,19},{19,3},{4,20},{20... | collective-permute-start | bytes 3145736 | tf_op jit(solution)/shard_map/ppermute | solution.py:26
  18.0 80.1 %copy-start.4 = (bf16[64,8192]{1,0:T(8,128)(2,1)}, bf16[64,8192]{1,0:T(8,128)(2,1)S(1)}, u32[]{:S(2)}) copy-start(bf16[64,8192]{1,0:T(8,128)(2,1)S(1)} %collective-permute-done.1.refs_2_) | copy-start | bytes 3145732
  18.0 36.2 %collective-permute-start.28 = (bf16[1024,512]{1,0:T(8,128)(2,1)}, bf16[1024,512]{1,0:T(8,128)(2,1)S(1)}, u32[]{:S(2)}, u32[]{:S(2)}) collective-permute-start(bf16[1024,512]{1,0:T(8,128)(2,1)} %refs_16_.7), channel_id=1, source_target_pairs={{0,1},{1,0},{2,3},{3,2},{4,5},{5,4},{6,7},{7,6},{8,9},{9,8},{10,11... | collective-permute-start | bytes 3145736 | tf_op jit(solution)/shard_map/ppermute | solution.py:26
  32.6 75.0 %copy-start = (bf16[64,8192]{1,0:T(8,128)(2,1)}, bf16[64,8192]{1,0:T(8,128)(2,1)S(1)}, u32[]{:S(2)}) copy-start(bf16[64,8192]{1,0:T(8,128)(2,1)S(1)} %collective-permute-done.7.refs_0_.refs_8_) | copy-start | bytes 3145732
  32.6 23.4 %collective-permute-start.2 = (bf16[64,8192]{1,0:T(8,128)(2,1)S(1)}, bf16[64,8192]{1,0:T(8,128)(2,1)S(1)}, u32[]{:S(2)}, u32[]{:S(2)}) collective-permute-start(bf16[64,8192]{1,0:T(8,128)(2,1)S(1)} %collective-permute-done.refs_1_), channel_id=1, source_target_pairs={{0,2},{1,7},{2,4},{3,1},{4,6},{5,3},{6,0},{7,5},{8,10},{9,15},{10,... | collective-permute-start | bytes 3145736 | tf_op jit(solution)/shard_map/ppermute | solution.py:35
  32.6 65.5 %copy-start.9 = (bf16[1024,512]{1,0:T(8,128)(2,1)}, bf16[1024,512]{1,0:T(8,128)(2,1)S(1)}, u32[]{:S(2)}) copy-start(bf16[1024,512]{1,0:T(8,128)(2,1)S(1)} %collective-permute-done.15.refs_9_.refs_7_.refs_17_) | copy-start | bytes 3145732
  32.6 26.1 %collective-permute-start.3 = (bf16[64,8192]{1,0:T(8,128)(2,1)S(1)}, bf16[64,8192]{1,0:T(8,128)(2,1)S(1)}, u32[]{:S(2)}, u32[]{:S(2)}) collective-permute-start(bf16[64,8192]{1,0:T(8,128)(2,1)S(1)} %collective-permute-done.1.refs_2_), channel_id=1, source_target_pairs={{0,1},{1,0},{2,3},{3,2},{4,5},{5,4},{6,7},{7,6},{8,9},{9,8},{10,11... | collective-permute-start | bytes 3145736 | tf_op jit(solution)/shard_map/ppermute | solution.py:26
  33.9 25.3 %collective-permute-start.5 = (bf16[64,8192]{1,0:T(8,128)(2,1)S(1)}, bf16[64,8192]{1,0:T(8,128)(2,1)}, u32[]{:S(2)}, u32[]{:S(2)}) collective-permute-start(bf16[64,8192]{1,0:T(8,128)(2,1)S(1)} %collective-permute-done.1.refs_2_), channel_id=1, source_target_pairs={{0,2},{1,7},{2,4},{3,1},{4,6},{5,3},{6,0},{7,5},{8,10},{9,15},{10,... | collective-permute-start | bytes 3145736 | tf_op jit(solution)/shard_map/ppermute | solution.py:35
  54.2 43.9 %copy-start.11 = (bf16[1024,512]{1,0:T(8,128)(2,1)}, bf16[1024,512]{1,0:T(8,128)(2,1)S(1)}, u32[]{:S(2)}) copy-start(bf16[1024,512]{1,0:T(8,128)(2,1)S(1)} %collective-permute-done.20.refs_20_) | copy-start | bytes 3145732
  54.2 4.9 %collective-permute-start.8 = (bf16[64,8192]{1,0:T(8,128)(2,1)S(1)}, bf16[64,8192]{1,0:T(8,128)(2,1)S(1)}, u32[]{:S(2)}, u32[]{:S(2)}) collective-permute-start(bf16[64,8192]{1,0:T(8,128)(2,1)S(1)} %collective-permute-done.7.refs_0_.refs_8_), channel_id=1, source_target_pairs={{0,1},{1,0},{2,3},{3,2},{4,5},{5,4},{6,7},{7,6},{8,9},{9,8},{10,11... | collective-permute-start | bytes 3145736 | tf_op jit(solution)/shard_map/ppermute | solution.py:26
  54.2 14.7 %collective-permute-start.9 = (bf16[64,8192]{1,0:T(8,128)(2,1)S(1)}, bf16[64,8192]{1,0:T(8,128)(2,1)S(1)}, u32[]{:S(2)}, u32[]{:S(2)}) collective-permute-start(bf16[64,8192]{1,0:T(8,128)(2,1)S(1)} %collective-permute-done.7.refs_0_.refs_8_), channel_id=1, source_target_pairs={{0,2},{1,7},{2,4},{3,1},{4,6},{5,3},{6,0},{7,5},{8,10},{9,15},{10,... | collective-permute-start | bytes 3145736 | tf_op jit(solution)/shard_map/ppermute | solution.py:35
  55.9 42.2 %copy-start.5 = (bf16[64,8192]{1,0:T(8,128)(2,1)}, bf16[64,8192]{1,0:T(8,128)(2,1)S(1)}, u32[]{:S(2)}) copy-start(bf16[64,8192]{1,0:T(8,128)(2,1)S(1)} %collective-permute-done.2.refs_3_) | copy-start | bytes 3145732
  55.9 15.2 %collective-permute-start.17 = (bf16[1024,512]{1,0:T(8,128)(2,1)S(1)}, bf16[1024,512]{1,0:T(8,128)(2,1)S(1)}, u32[]{:S(2)}, u32[]{:S(2)}) collective-permute-start(bf16[1024,512]{1,0:T(8,128)(2,1)S(1)} %collective-permute-done.16), channel_id=1, source_target_pairs={{0,32},{1,97},{32,64},{33,1},{64,96},{65,33},{96,0},{97,65},{2,34}... | collective-permute-start | bytes 3145736 | tf_op jit(solution)/shard_map/ppermute | solution.py:35
  58.7 39.4 %copy-start.6 = (bf16[64,8192]{1,0:T(8,128)(2,1)}, bf16[64,8192]{1,0:T(8,128)(2,1)S(1)}, u32[]{:S(2)}) copy-start(bf16[64,8192]{1,0:T(8,128)(2,1)S(1)} %collective-permute-done.3.refs_4_) | copy-start | bytes 3145732
  58.7 23.0 %collective-permute-start.19 = (bf16[1024,512]{1,0:T(8,128)(2,1)S(1)}, bf16[1024,512]{1,0:T(8,128)(2,1)S(1)}, u32[]{:S(2)}, u32[]{:S(2)}) collective-permute-start(bf16[1024,512]{1,0:T(8,128)(2,1)S(1)} %collective-permute-done.15.refs_9_.refs_7_.refs_17_), channel_id=1, source_target_pairs={{0,32},{1,97},{32,64},{33,1},{64,96},{65,33},{96,0},{97,65},{2,34}... | collective-permute-start | bytes 3145736 | tf_op jit(solution)/shard_map/ppermute | solution.py:35
  59.2 22.9 %collective-permute-start.22 = (bf16[1024,512]{1,0:T(8,128)(2,1)S(1)}, bf16[1024,512]{1,0:T(8,128)(2,1)}, u32[]{:S(2)}, u32[]{:S(2)}) collective-permute-start(bf16[1024,512]{1,0:T(8,128)(2,1)S(1)} %collective-permute-done.20.refs_20_), channel_id=1, source_target_pairs={{0,1},{1,0},{2,3},{3,2},{4,5},{5,4},{6,7},{7,6},{8,9},{9,8},{10,11... | collective-permute-start | bytes 3145736 | tf_op jit(solution)/shard_map/ppermute | solution.py:26
  59.2 48.4 %copy-start.1 = (bf16[64,8192]{1,0:T(8,128)(2,1)}, bf16[64,8192]{1,0:T(8,128)(2,1)S(1)}, u32[]{:S(2)}) copy-start(bf16[64,8192]{1,0:T(8,128)(2,1)S(1)} %collective-permute-done.8.refs_1_.refs_9_) | copy-start | bytes 3145732
  59.2 23.0 %collective-permute-start.4 = (bf16[64,8192]{1,0:T(8,128)(2,1)S(1)}, bf16[64,8192]{1,0:T(8,128)(2,1)S(1)}, u32[]{:S(2)}, u32[]{:S(2)}) collective-permute-start(bf16[64,8192]{1,0:T(8,128)(2,1)S(1)} %collective-permute-done.2.refs_3_), channel_id=1, source_target_pairs={{0,1},{1,0},{2,3},{3,2},{4,5},{5,4},{6,7},{7,6},{8,9},{9,8},{10,11... | collective-permute-start | bytes 3145736 | tf_op jit(solution)/shard_map/ppermute | solution.py:26
  69.0 38.6 %copy-start.2 = (bf16[64,8192]{1,0:T(8,128)(2,1)}, bf16[64,8192]{1,0:T(8,128)(2,1)S(1)}, u32[]{:S(2)}) copy-start(bf16[64,8192]{1,0:T(8,128)(2,1)S(1)} %collective-permute-done.9.refs_2_.refs_10_) | copy-start | bytes 3145732
  69.0 16.7 %collective-permute-start.10 = (bf16[64,8192]{1,0:T(8,128)(2,1)S(1)}, bf16[64,8192]{1,0:T(8,128)(2,1)}, u32[]{:S(2)}, u32[]{:S(2)}) collective-permute-start(bf16[64,8192]{1,0:T(8,128)(2,1)S(1)} %collective-permute-done.8.refs_1_.refs_9_), channel_id=1, source_target_pairs={{0,2},{1,7},{2,4},{3,1},{4,6},{5,3},{6,0},{7,5},{8,10},{9,15},{10,... | collective-permute-start | bytes 3145736 | tf_op jit(solution)/shard_map/ppermute | solution.py:35
  71.1 27.0 %copy-start.16 = (bf16[1024,512]{1,0:T(8,128)(2,1)}, bf16[1024,512]{1,0:T(8,128)(2,1)S(1)}, u32[]{:S(2)}) copy-start(bf16[1024,512]{1,0:T(8,128)(2,1)S(1)} %collective-permute-done.17) | copy-start | bytes 3145732
  71.1 23.2 %collective-permute-start.13 = (bf16[64,8192]{1,0:T(8,128)(2,1)S(1)}, bf16[64,8192]{1,0:T(8,128)(2,1)}, u32[]{:S(2)}, u32[]{:S(2)}) collective-permute-start(bf16[64,8192]{1,0:T(8,128)(2,1)S(1)} %collective-permute-done.9.refs_2_.refs_10_), channel_id=1, source_target_pairs={{0,2},{1,7},{2,4},{3,1},{4,6},{5,3},{6,0},{7,5},{8,10},{9,15},{10,... | collective-permute-start | bytes 3145736 | tf_op jit(solution)/shard_map/ppermute | solution.py:35
  81.7 17.1 %collective-permute-start.6 = (bf16[64,8192]{1,0:T(8,128)(2,1)}, bf16[64,8192]{1,0:T(8,128)(2,1)}, u32[]{:S(2)}, u32[]{:S(2)}) collective-permute-start(bf16[64,8192]{1,0:T(8,128)(2,1)} %collective-permute-done.5.refs_6_), channel_id=1, source_target_pairs={{0,1},{1,0},{2,3},{3,2},{4,5},{5,4},{6,7},{7,6},{8,9},{9,8},{10,11... | collective-permute-start | bytes 3145736 | tf_op jit(solution)/shard_map/ppermute | solution.py:26
  82.1 20.4 %collective-permute-start.11 = (bf16[64,8192]{1,0:T(8,128)(2,1)S(1)}, bf16[64,8192]{1,0:T(8,128)(2,1)}, u32[]{:S(2)}, u32[]{:S(2)}) collective-permute-start(bf16[64,8192]{1,0:T(8,128)(2,1)S(1)} %collective-permute-done.9.refs_2_.refs_10_), channel_id=1, source_target_pairs={{0,1},{1,0},{2,3},{3,2},{4,5},{5,4},{6,7},{7,6},{8,9},{9,8},{10,11... | collective-permute-start | bytes 3145736 | tf_op jit(solution)/shard_map/ppermute | solution.py:26
  82.2 23.1 %collective-permute-start.23 = (bf16[1024,512]{1,0:T(8,128)(2,1)}, bf16[1024,512]{1,0:T(8,128)(2,1)}, u32[]{:S(2)}, u32[]{:S(2)}) collective-permute-start(bf16[1024,512]{1,0:T(8,128)(2,1)} %collective-permute-done.22), channel_id=1, source_target_pairs={{0,32},{1,97},{32,64},{33,1},{64,96},{65,33},{96,0},{97,65},{2,34}... | collective-permute-start | bytes 3145736 | tf_op jit(solution)/shard_map/ppermute | solution.py:35
  85.7 20.7 %collective-permute-start.12 = (bf16[64,8192]{1,0:T(8,128)(2,1)}, bf16[64,8192]{1,0:T(8,128)(2,1)}, u32[]{:S(2)}, u32[]{:S(2)}) collective-permute-start(bf16[64,8192]{1,0:T(8,128)(2,1)} %collective-permute-done.10.refs_3_.refs_11_), channel_id=1, source_target_pairs={{0,1},{1,0},{2,3},{3,2},{4,5},{5,4},{6,7},{7,6},{8,9},{9,8},{10,11... | collective-permute-start | bytes 3145736 | tf_op jit(solution)/shard_map/ppermute | solution.py:26
  94.3 13.3 %collective-permute-start.14 = (bf16[64,8192]{1,0:T(8,128)(2,1)}, bf16[64,8192]{1,0:T(8,128)(2,1)}, u32[]{:S(2)}, u32[]{:S(2)}) collective-permute-start(bf16[64,8192]{1,0:T(8,128)(2,1)} %collective-permute-done.13.refs_14_), channel_id=1, source_target_pairs={{0,1},{1,0},{2,3},{3,2},{4,5},{5,4},{6,7},{7,6},{8,9},{9,8},{10,11... | collective-permute-start | bytes 3145736 | tf_op jit(solution)/shard_map/ppermute | solution.py:26
  98.8 17.2 %collective-permute-start.18 = (bf16[1024,512]{1,0:T(8,128)(2,1)}, bf16[1024,512]{1,0:T(8,128)(2,1)}, u32[]{:S(2)}, u32[]{:S(2)}) collective-permute-start(bf16[1024,512]{1,0:T(8,128)(2,1)} %copy-done.16), channel_id=1, source_target_pairs={{0,1},{1,0},{2,3},{3,2},{4,5},{5,4},{6,7},{7,6},{8,9},{9,8},{10,11... | collective-permute-start | bytes 3145736 | tf_op jit(solution)/shard_map/ppermute | solution.py:26
  102.5 34.5 %collective-permute-start.21 = (bf16[1024,512]{1,0:T(8,128)(2,1)}, bf16[1024,512]{1,0:T(8,128)(2,1)}, u32[]{:S(2)}, u32[]{:S(2)}) collective-permute-start(bf16[1024,512]{1,0:T(8,128)(2,1)} %copy-done.11), channel_id=1, source_target_pairs={{0,32},{1,97},{32,64},{33,1},{64,96},{65,33},{96,0},{97,65},{2,34}... | collective-permute-start | bytes 3145736 | tf_op jit(solution)/shard_map/ppermute | solution.py:35
  105.2 33.4 %collective-permute-start.25 = (bf16[1024,512]{1,0:T(8,128)(2,1)}, bf16[1024,512]{1,0:T(8,128)(2,1)}, u32[]{:S(2)}, u32[]{:S(2)}) collective-permute-start(bf16[1024,512]{1,0:T(8,128)(2,1)} %copy-done.10), channel_id=1, source_target_pairs={{0,16},{16,0},{1,17},{17,1},{2,18},{18,2},{3,19},{19,3},{4,20},{20... | collective-permute-start | bytes 3145736 | tf_op jit(solution)/shard_map/ppermute | solution.py:26
  106.4 32.7 %collective-permute-start.24 = (bf16[1024,512]{1,0:T(8,128)(2,1)}, bf16[1024,512]{1,0:T(8,128)(2,1)}, u32[]{:S(2)}, u32[]{:S(2)}) collective-permute-start(bf16[1024,512]{1,0:T(8,128)(2,1)} %collective-permute-done.23), channel_id=1, source_target_pairs={{0,1},{1,0},{2,3},{3,2},{4,5},{5,4},{6,7},{7,6},{8,9},{9,8},{10,11... | collective-permute-start | bytes 3145736 | tf_op jit(solution)/shard_map/ppermute | solution.py:26
  114.7 35.5 %collective-permute-start.32 = (bf16[1024,512]{1,0:T(8,128)(2,1)}, bf16[1024,512]{1,0:T(8,128)(2,1)}, u32[]{:S(2)}, u32[]{:S(2)}) collective-permute-start(bf16[1024,512]{1,0:T(8,128)(2,1)} %get-tuple-element.28), channel_id=1, source_target_pairs={{0,32},{1,97},{32,64},{33,1},{64,96},{65,33},{96,0},{97,65},{2,34}... | collective-permute-start | bytes 3145736 | tf_op jit(solution)/shard_map/ppermute | solution.py:35
  122.4 35.2 %collective-permute-start.35 = (bf16[1024,512]{1,0:T(8,128)(2,1)S(1)}, bf16[1024,512]{1,0:T(8,128)(2,1)S(1)}, u32[]{:S(2)}, u32[]{:S(2)}) collective-permute-start(bf16[1024,512]{1,0:T(8,128)(2,1)S(1)} %copy-done.17), channel_id=1, source_target_pairs={{0,16},{16,0},{1,17},{17,1},{2,18},{18,2},{3,19},{19,3},{4,20},{20... | collective-permute-start | bytes 3145736 | tf_op jit(solution)/shard_map/ppermute | solution.py:26
  137.0 40.4 %collective-permute-start.31 = (bf16[1024,512]{1,0:T(8,128)(2,1)}, bf16[1024,512]{1,0:T(8,128)(2,1)}, u32[]{:S(2)}, u32[]{:S(2)}) collective-permute-start(bf16[1024,512]{1,0:T(8,128)(2,1)} %get-tuple-element.27), channel_id=1, source_target_pairs={{0,32},{1,97},{32,64},{33,1},{64,96},{65,33},{96,0},{97,65},{2,34}... | collective-permute-start | bytes 3145736 | tf_op jit(solution)/shard_map/ppermute | solution.py:35
  138.6 38.3 %collective-permute-start.29 = (bf16[1024,512]{1,0:T(8,128)(2,1)}, bf16[1024,512]{1,0:T(8,128)(2,1)}, u32[]{:S(2)}, u32[]{:S(2)}) collective-permute-start(bf16[1024,512]{1,0:T(8,128)(2,1)} %get-tuple-element.25), channel_id=1, source_target_pairs={{0,32},{1,97},{32,64},{33,1},{64,96},{65,33},{96,0},{97,65},{2,34}... | collective-permute-start | bytes 3145736 | tf_op jit(solution)/shard_map/ppermute | solution.py:35
  150.2 27.2 %collective-permute-start.33 = (bf16[1024,512]{1,0:T(8,128)(2,1)}, bf16[1024,512]{1,0:T(8,128)(2,1)}, u32[]{:S(2)}, u32[]{:S(2)}) collective-permute-start(bf16[1024,512]{1,0:T(8,128)(2,1)} %collective-permute-done.32), channel_id=1, source_target_pairs={{0,1},{1,0},{2,3},{3,2},{4,5},{5,4},{6,7},{7,6},{8,9},{9,8},{10,11... | collective-permute-start | bytes 3145736 | tf_op jit(solution)/shard_map/ppermute | solution.py:26
  157.9 24.2 %collective-permute-start.36 = (bf16[1024,512]{1,0:T(8,128)(2,1)S(1)}, bf16[1024,512]{1,0:T(8,128)(2,1)S(1)}, u32[]{:S(2)}, u32[]{:S(2)}) collective-permute-start(bf16[1024,512]{1,0:T(8,128)(2,1)S(1)} %add_convert_fusion.2), channel_id=1, source_target_pairs={{0,32},{1,97},{32,64},{33,1},{64,96},{65,33},{96,0},{97,65},{2,34}... | collective-permute-start | bytes 3145736 | tf_op jit(solution)/shard_map/ppermute | solution.py:35
  168.7 13.3 %collective-permute-start.26 = (bf16[128,1024]{1,0:T(8,128)(2,1)}, bf16[128,1024]{1,0:T(8,128)(2,1)S(1)}, u32[]{:S(2)}, u32[]{:S(2)}) collective-permute-start(bf16[128,1024]{1,0:T(8,128)(2,1)} %get-tuple-element.23), channel_id=1, source_target_pairs={{0,1},{1,0},{2,3},{3,2},{4,5},{5,4},{6,7},{7,6},{8,9},{9,8},{10,11... | collective-permute-start | bytes 786440 | tf_op jit(solution)/shard_map/ppermute | solution.py:26
  176.9 12.5 %collective-permute-start.30 = (bf16[1024,512]{1,0:T(8,128)(2,1)}, bf16[1024,512]{1,0:T(8,128)(2,1)}, u32[]{:S(2)}, u32[]{:S(2)}) collective-permute-start(bf16[1024,512]{1,0:T(8,128)(2,1)} %collective-permute-done.29), channel_id=1, source_target_pairs={{0,1},{1,0},{2,3},{3,2},{4,5},{5,4},{6,7},{7,6},{8,9},{9,8},{10,11... | collective-permute-start | bytes 3145736 | tf_op jit(solution)/shard_map/ppermute | solution.py:26
  180.8 25.0 %collective-permute-start.34 = (bf16[1024,512]{1,0:T(8,128)(2,1)}, bf16[1024,512]{1,0:T(8,128)(2,1)}, u32[]{:S(2)}, u32[]{:S(2)}) collective-permute-start(bf16[1024,512]{1,0:T(8,128)(2,1)} %add_convert_fusion.3), channel_id=1, source_target_pairs={{0,16},{16,0},{1,17},{17,1},{2,18},{18,2},{3,19},{19,3},{4,20},{20... | collective-permute-start | bytes 3145736 | tf_op jit(solution)/shard_map/ppermute | solution.py:26
  183.4 24.4 %collective-permute-start.37 = (bf16[1024,512]{1,0:T(8,128)(2,1)}, bf16[1024,512]{1,0:T(8,128)(2,1)S(1)}, u32[]{:S(2)}, u32[]{:S(2)}) collective-permute-start(bf16[1024,512]{1,0:T(8,128)(2,1)} %add_convert_fusion.1), channel_id=1, source_target_pairs={{0,32},{1,97},{32,64},{33,1},{64,96},{65,33},{96,0},{97,65},{2,34}... | collective-permute-start | bytes 3145736 | tf_op jit(solution)/shard_map/ppermute | solution.py:35
  183.9 4.9 %collective-permute-start.27 = (bf16[2,32,1024]{2,1,0:T(8,128)(2,1)S(1)}, bf16[2,32,1024]{2,1,0:T(8,128)(2,1)S(1)}, u32[]{:S(2)}, u32[]{:S(2)}) collective-permute-start(bf16[2,32,1024]{2,1,0:T(8,128)(2,1)S(1)} %fusion.1), channel_id=1, source_target_pairs={{0,2},{2,0},{4,6},{6,4},{1,3},{3,1},{5,7},{7,5},{8,10},{10,8},{12,... | collective-permute-start | bytes 393224 | tf_op jit(solution)/shard_map/ppermute | solution.py:417
  (8 other events, 85.3 us)
